TPU v7x, 1024 devices: a whole 4x4x32 slice. The times are simulated.
1024 devices in a mesh: dp: 64 (over y, z_lo, core), tensor: 16 (over x, z_hi).
Axes of the slice: x: 4, y: 4, z: 32 (z_hi: 4, z_lo: 8; z = z_hi * 8 + z_lo), core: 2. Of those that a mesh axis runs over, the one named last changes fastest.
Arguments:
- hidden_in: bfloat16 [64, 128, 16384], P('dp'), may hold values from -16 to 16
- value_weight: bfloat16 [16384, 1024], P(None, 'tensor'), may hold values from -0.046875 to 0.046875
- queries: bfloat16 [64, 128, 16384], P('dp', None, 'tensor'), may hold values from -4 to 4
- key_rows: bfloat16 [64, 128, 1024], P('dp', None, 'tensor'), may hold values from -4 to 4
- attention_out: bfloat16 [64, 128, 16384], P('dp', None, 'tensor'), may hold values from -4 to 4
- output_grad: bfloat16 [64, 128, 16384], P('dp', None, 'tensor'), may hold values from -6 to 6
- log_normalizer: float32 [64, 128, 128], P('dp', None, 'tensor'), may hold values from 1 to 5
- document_ids: int32 [64, 128], P('dp'), may hold values from 0 to 3, never falling along the last dimension, each value on 1 to 64 neighbouring positions
Outputs:
- query_grad: bfloat16 [64, 128, 16384], P('dp', None, 'tensor')
- key_grad: bfloat16 [64, 128, 1024], P('dp', None, 'tensor')
- input_grad: bfloat16 [64, 128, 16384], P('dp', 'tensor')
- value_weight_grad: float32 [16384, 1024], P('dp', 'tensor')
Inputs may be any that keep to these rules, and one draw needn't show every extreme that they name: `document_ids`: within one group the ids never fall; all 4 documents occur, each of 1 to 64 tokens.
All inputs are finite; a program needn't handle non-finite values.
Results may differ from a plain program's by a relative error of at most 0.014.
Values may be sent and summed in bfloat16 or wider, within the bound.
A program may use at most 64 MiB of HBM per device.

v0:
```python
import math

import jax
import jax.numpy as jnp
from jax import lax
from jax.sharding import Mesh
from jax.sharding import PartitionSpec as P

TENSOR = ("tensor_0", "tensor_1")
DP = ("dp_0", "dp_1", "dp_2")


def partner(value, axis, distance):
    mask = 2**distance
    pairs = [(source, source ^ mask) for source in range(lax.axis_size(axis))]
    return lax.ppermute(value, axis, pairs)


def sum_by_axis(terms, axes):
    running = terms.astype(jnp.bfloat16)
    for axis in axes:
        running = lax.psum_scatter(running, axis, scatter_dimension=0, tiled=True)
    return running.astype(jnp.float32)


def cut_along(value, dim, count):
    shape = value.shape
    pieces = value.reshape(*shape[:dim], count, shape[dim] // count, *shape[dim + 1 :])
    return jnp.moveaxis(pieces, dim, 0)


def sum_by_chip(value, chips, core, dim):
    sizes = (lax.axis_size(chips), lax.axis_size(core))
    pieces = cut_along(value, dim, sizes[0] * sizes[1])
    inside = pieces.shape[1:]
    pieces = pieces.reshape(*sizes, *inside).swapaxes(0, 1).reshape(-1, *inside)
    pieces = lax.psum_scatter(pieces, core, scatter_dimension=0, tiled=True)
    return lax.psum_scatter(pieces, chips, scatter_dimension=0, tiled=True)[0]


def per_device(
    hidden_in,
    value_weight,
    queries,
    key_rows,
    attention_out,
    output_grad,
    log_normalizer,
    document_ids,
):
    tokens = hidden_in.shape[1]
    head_count = log_normalizer.shape[2]
    half_width = key_rows.shape[2]
    head_width = 2 * half_width
    score_scale = 1.0 / math.sqrt(head_width)
    inputs_local = hidden_in[0]
    value_half = jnp.dot(inputs_local, value_weight, preferred_element_type=jnp.float32).astype(
        jnp.bfloat16
    )
    key_half = key_rows[0]
    other_key, other_value = partner((key_half, value_half), TENSOR, 0)
    pair_member = lax.axis_index(TENSOR) % 2
    lower_member = pair_member == 0
    keys_full = jnp.where(
        lower_member,
        jnp.concatenate([key_half, other_key], 1),
        jnp.concatenate([other_key, key_half], 1),
    )
    values_full = jnp.where(
        lower_member,
        jnp.concatenate([value_half, other_value], 1),
        jnp.concatenate([other_value, value_half], 1),
    )
    query_heads = queries[0].reshape(tokens, head_count, head_width)
    grad_heads = output_grad[0].reshape(tokens, head_count, head_width)
    out_heads = attention_out[0].reshape(tokens, head_count, head_width)
    position = jnp.arange(tokens, dtype=jnp.int32)
    documents = document_ids[0]
    allowed = (position[None, :] <= position[:, None]) & (documents[:, None] == documents[None, :])
    scores = (
        jnp.einsum("thd,sd->hts", query_heads, keys_full, preferred_element_type=jnp.float32)
        * score_scale
    )
    normalizers = jnp.transpose(log_normalizer[0])[:, :, None]
    probabilities = jnp.where(allowed[None], jnp.exp(scores - normalizers), 0.0)
    probs_low = probabilities.astype(jnp.bfloat16)
    value_part = jnp.einsum(
        "hts,thd->sd", probs_low, grad_heads, preferred_element_type=jnp.float32
    )
    row_dots = jnp.einsum("thd,thd->ht", grad_heads, out_heads, preferred_element_type=jnp.float32)
    prob_grad = jnp.einsum(
        "thd,sd->hts", grad_heads, values_full, preferred_element_type=jnp.float32
    )
    score_grad = (probabilities * (prob_grad - row_dots[:, :, None]) * score_scale).astype(
        jnp.bfloat16
    )
    query_grad = jnp.einsum(
        "hts,sd->thd", score_grad, keys_full, preferred_element_type=jnp.float32
    )
    query_grad = query_grad.astype(jnp.bfloat16).reshape(1, tokens, head_count * head_width)
    key_part = jnp.einsum(
        "hts,thd->sd", score_grad, query_heads, preferred_element_type=jnp.float32
    )
    own_offset = pair_member * half_width
    other_offset = (1 - pair_member) * half_width
    send_key = lax.dynamic_slice_in_dim(key_part, other_offset, half_width, 1)
    send_value = lax.dynamic_slice_in_dim(value_part, other_offset, half_width, 1)
    got_key, got_value = partner((send_key, send_value), TENSOR, 0)
    key_sum = lax.dynamic_slice_in_dim(key_part, own_offset, half_width, 1) + got_key
    value_sum = lax.dynamic_slice_in_dim(value_part, own_offset, half_width, 1) + got_value
    key_grad = key_sum.astype(jnp.bfloat16).reshape(1, tokens, half_width)
    value_grad = value_sum.astype(jnp.bfloat16)
    input_sum = sum_by_axis(
        lax.dot_general(
            value_grad, value_weight, (((1,), (1,)), ((), ())), preferred_element_type=jnp.float32
        ),
        TENSOR,
    )
    weight_grad = sum_by_chip(
        lax.dot_general(
            inputs_local, value_grad, (((0,), (0,)), ((), ())), preferred_element_type=jnp.float32
        ),
        ("dp_0", "dp_1"),
        "dp_2",
        0,
    )
    input_grad = input_sum.astype(jnp.bfloat16).reshape((1,) + input_sum.shape)
    return (query_grad, key_grad, input_grad, weight_grad)


def solution(mesh):
    finer = Mesh(
        mesh.devices.reshape(4, 8, 2, 4, 4), ("dp_0", "dp_1", "dp_2", "tensor_0", "tensor_1")
    )
    return jax.shard_map(
        per_device,
        mesh=finer,
        in_specs=(
            P(DP, None, None),
            P(None, TENSOR),
            P(DP, None, TENSOR),
            P(DP, None, TENSOR),
            P(DP, None, TENSOR),
            P(DP, None, TENSOR),
            P(DP, None, TENSOR),
            P(DP, None),
        ),
        out_specs=(P(DP, None, TENSOR), P(DP, None, TENSOR), P(DP, TENSOR, None), P(DP, TENSOR)),
        check_vma=False,
    )
```

profile of v0, /device:TPU:2, one launch (start us, length us, event | category | flops | bytes accessed | tf_op | source)
XLA Modules:
  0.0 532.9 jit_solution(9868931789772908534)
XLA Ops:
  7.2 0.0 copy-start
  7.2 0.0 reduce-scatter.5.cloned.1.call-start
  7.2 15.9 %collective-permute-start = (bf16[128,64]{0,1:T(8,128)(2,1)}, bf16[128,64]{0,1:T(8,128)(2,1)S(1)}, u32[]{:S(2)}, u32[]{:S(2)}) collective-permute-start(bf16[128,64]{0,1:T(8,128)(2,1)} %bitcast.86), channel_id=1, source_target_pairs={{0,1},{1,0},{2,3},{3,2},{4,5},{5,4},{6,7},{7,6},{8,9},{9,8},{10,11... | collective-permute-start | bytes 49160 | tf_op jit(solution)/shard_map/ppermute | solution.py:16
  23.1 0.8 fusion.16
  23.9 1.1 copy.38
  25.1 1.0 copy.39
  26.1 0.2 copy.20
  26.3 0.0 collective-permute-done
  26.3 1.1 fusion.7
  27.4 0.2 convolution_bitcast_fusion.2
  27.6 11.3 %collective-permute-start.3 = (f32[128,64]{0,1:T(8,128)S(1)}, f32[128,64]{0,1:T(8,128)S(1)}, u32[]{:S(2)}, u32[]{:S(2)}) collective-permute-start(f32[128,64]{0,1:T(8,128)S(1)} %constant_dynamic-slice_fusion), channel_id=1, source_target_pairs={{0,1},{1,0},{2,3},{3,2},{4,5},{5,4},{6,7},{7,6},{8,9},{9,8},{10,11... | collective-permute-start | bytes 98312 | tf_op jit(solution)/shard_map/ppermute | solution.py:16
  39.0 3.5 collective-permute-done.3
  42.5 0.0 copy-done
  42.5 3.2 convolution_convert_fusion
  45.7 0.0 reduce-scatter.5.cloned.1.call-update
  45.7 0.0 reduce-scatter.9.cloned.1.call-start
  45.8 4.9 convolution_bitcast_fusion
  50.6 6.6 %reshape_reshape.3 = f32[32,2,256,64]{2,1,0,3:T(2,128)} reshape(f32[16384,64]{0,1:T(8,128)} %convolution_bitcast_fusion) | data formatting | bytes 8388608 | tf_op jit(solution)/shard_map/reshape;reshape | solution.py:36
  57.2 6.6 %copy.21 = f32[2,32,256,64]{2,3,1,0:T(8,128)} copy(f32[2,32,256,64]{2,0,1,3:T(2,128)} %bitcast.77) | data formatting | bytes 8388608 | tf_op jit(solution)/shard_map/transpose | solution.py:36
  63.8 0.0 reduce-scatter.9.cloned.1.call-update
  63.8 0.0 reduce-scatter.7.cloned.1.call-start
  63.9 51.8 %reduce-scatter.5.cloned.1.call-done = bf16[32,16384]{1,0:T(8,128)(2,1)} async-done(((bf16[128,16384]{1,0:T(8,128)(2,1)}), bf16[32,16384]{1,0:T(8,128)(2,1)}) %reduce-scatter.5.cloned.1.call-update) | async-done | bytes 1048592 | tf_op jit(solution)/shard_map/reduce_scatter | solution.py:22
  115.7 0.0 reduce-scatter.7.cloned.1.call-update
  115.7 0.0 reduce-scatter.11.cloned.1.call-start
  115.7 37.4 %reduce-scatter.9.cloned.1.call-done = f32[32,256,64]{1,2,0:T(8,128)} async-done(((f32[64,256,64]{1,2,0:T(8,128)}), f32[32,256,64]{1,2,0:T(8,128)}) %reduce-scatter.9.cloned.1.call-update) | async-done | bytes 2097168 | tf_op jit(solution)/shard_map/reduce_scatter | solution.py:37
  153.1 0.0 reduce-scatter.11.cloned.1.call-update
  153.1 0.0 copy-start.1
  153.1 0.0 copy-start.2
  153.1 3.8 fusion.11
  156.9 12.8 %collective-permute-start.1 = (bf16[128,64]{0,1:T(8,128)(2,1)S(1)}, bf16[128,64]{0,1:T(8,128)(2,1)S(1)}, u32[]{:S(2)}, u32[]{:S(2)}) collective-permute-start(bf16[128,64]{0,1:T(8,128)(2,1)S(1)} %fusion.11), channel_id=1, source_target_pairs={{0,1},{1,0},{2,3},{3,2},{4,5},{5,4},{6,7},{7,6},{8,9},{9,8},{10,11... | collective-permute-start | bytes 49160 | tf_op jit(solution)/shard_map/ppermute | solution.py:16
  169.8 0.0 copy-done.1
  169.8 0.2 fusion.14
  170.1 1.4 collective-permute-done.1
  171.5 0.3 fusion.10
  171.7 0.2 convolution_bitcast_fusion.3
  172.0 12.8 %collective-permute-start.2 = (f32[128,64]{0,1:T(8,128)S(1)}, f32[128,64]{0,1:T(8,128)S(1)}, u32[]{:S(2)}, u32[]{:S(2)}) collective-permute-start(f32[128,64]{0,1:T(8,128)S(1)} %constant_dynamic-slice_fusion.1), channel_id=1, source_target_pairs={{0,1},{1,0},{2,3},{3,2},{4,5},{5,4},{6,7},{7,6},{8,9},{9,8},{10,11... | collective-permute-start | bytes 98312 | tf_op jit(solution)/shard_map/ppermute | solution.py:16
  184.8 0.0 copy-done.2
  184.8 0.2 convolution_convert_fusion.1
  185.0 0.9 copy.22
  185.9 0.8 collective-permute-done.2
  186.7 0.6 fusion.28
  187.3 86.8 %reduce-scatter.7.cloned.1.call-done = bf16[8,16384]{1,0:T(8,128)(2,1)} async-done(((bf16[32,16384]{1,0:T(8,128)(2,1)}), bf16[8,16384]{1,0:T(8,128)(2,1)}) %reduce-scatter.7.cloned.1.call-update) | async-done | bytes 262160 | tf_op jit(solution)/shard_map/reduce_scatter | solution.py:22
  274.1 252.3 %reduce-scatter.11.cloned.1.call-done = f32[1,256,64]{1,2,0:T(8,128)} async-done(((f32[32,256,64]{1,2,0:T(8,128)}), f32[1,256,64]{1,2,0:T(8,128)}) %reduce-scatter.11.cloned.1.call-update) | async-done | bytes 65552 | tf_op jit(solution)/shard_map/reduce_scatter | solution.py:38
  (5 shorter events, 0.1 us)
Async XLA Ops:
  7.2 35.3 %copy-start = (bf16[16384,64]{0,1:T(8,128)(2,1)S(1)}, bf16[16384,64]{0,1:T(8,128)(2,1)}, u32[]{:S(2)}) copy-start(bf16[16384,64]{0,1:T(8,128)(2,1)} %param.9) | copy-start | bytes 6291460
  7.2 108.5 %reduce-scatter.5.cloned.1.call-start = ((), (), s32[]{:S(2)}) async-start(), calls=%async_computation.4 | async-start | bytes 5242880 | tf_op jit(solution)/shard_map/reduce_scatter | solution.py:22
  7.2 19.1 %collective-permute-start = (bf16[128,64]{0,1:T(8,128)(2,1)}, bf16[128,64]{0,1:T(8,128)(2,1)S(1)}, u32[]{:S(2)}, u32[]{:S(2)}) collective-permute-start(bf16[128,64]{0,1:T(8,128)(2,1)} %bitcast.86), channel_id=1, source_target_pairs={{0,1},{1,0},{2,3},{3,2},{4,5},{5,4},{6,7},{7,6},{8,9},{9,8},{10,11... | collective-permute-start | bytes 49160 | tf_op jit(solution)/shard_map/ppermute | solution.py:16
  27.6 14.8 %collective-permute-start.3 = (f32[128,64]{0,1:T(8,128)S(1)}, f32[128,64]{0,1:T(8,128)S(1)}, u32[]{:S(2)}, u32[]{:S(2)}) collective-permute-start(f32[128,64]{0,1:T(8,128)S(1)} %constant_dynamic-slice_fusion), channel_id=1, source_target_pairs={{0,1},{1,0},{2,3},{3,2},{4,5},{5,4},{6,7},{7,6},{8,9},{9,8},{10,11... | collective-permute-start | bytes 98312 | tf_op jit(solution)/shard_map/ppermute | solution.py:16
  45.7 107.4 %reduce-scatter.9.cloned.1.call-start = ((), (), s32[]{:S(2)}) async-start(), calls=%async_computation.6 | async-start | bytes 6291456 | tf_op jit(solution)/shard_map/reduce_scatter | solution.py:37
  63.8 210.3 %reduce-scatter.7.cloned.1.call-start = ((), (), s32[]{:S(2)}) async-start(), calls=%async_computation.5 | async-start | bytes 1310720 | tf_op jit(solution)/shard_map/reduce_scatter | solution.py:22
  115.7 410.7 %reduce-scatter.11.cloned.1.call-start = ((), (), s32[]{:S(2)}) async-start(), calls=%async_computation.7 | async-start | bytes 2162688 | tf_op jit(solution)/shard_map/reduce_scatter | solution.py:38
  153.1 16.6 %copy-start.1 = (bf16[1,128,1024]{2,1,0:T(8,128)(2,1)S(1)}, bf16[1,128,1024]{2,1,0:T(8,128)(2,1)}, u32[]{:S(2)}) copy-start(bf16[1,128,1024]{2,1,0:T(8,128)(2,1)} %param.12) | copy-start | bytes 786436
  153.1 31.6 %copy-start.2 = (bf16[1,128,64]{1,2,0:T(8,128)(2,1)S(1)}, bf16[1,128,64]{1,2,0:T(8,128)(2,1)}, u32[]{:S(2)}) copy-start(bf16[1,128,64]{1,2,0:T(8,128)(2,1)} %param.11) | copy-start | bytes 49156
  156.9 14.5 %collective-permute-start.1 = (bf16[128,64]{0,1:T(8,128)(2,1)S(1)}, bf16[128,64]{0,1:T(8,128)(2,1)S(1)}, u32[]{:S(2)}, u32[]{:S(2)}) collective-permute-start(bf16[128,64]{0,1:T(8,128)(2,1)S(1)} %fusion.11), channel_id=1, source_target_pairs={{0,1},{1,0},{2,3},{3,2},{4,5},{5,4},{6,7},{7,6},{8,9},{9,8},{10,11... | collective-permute-start | bytes 49160 | tf_op jit(solution)/shard_map/ppermute | solution.py:16
  172.0 14.7 %collective-permute-start.2 = (f32[128,64]{0,1:T(8,128)S(1)}, f32[128,64]{0,1:T(8,128)S(1)}, u32[]{:S(2)}, u32[]{:S(2)}) collective-permute-start(f32[128,64]{0,1:T(8,128)S(1)} %constant_dynamic-slice_fusion.1), channel_id=1, source_target_pairs={{0,1},{1,0},{2,3},{3,2},{4,5},{5,4},{6,7},{7,6},{8,9},{9,8},{10,11... | collective-permute-start | bytes 98312 | tf_op jit(solution)/shard_map/ppermute | solution.py:16
Sparse Core Ops, SparseCore 0:
  45.8 69.7 reduce-scatter.4
  119.1 33.9 reduce-scatter.8
  157.1 116.9 reduce-scatter.6
  277.9 248.4 reduce-scatter.10
where the time goes:
time: 533 us
  waiting for transfers between devices  434 us (81%)
  starting transfers between devices  52.9 us (10%)
  local copies, waits for them, and re-layouts  16.5 us (3%)
  between operations  14 us (3%)
  matrix products  13.9 us (3%)
    reduce_scatter x1, waiting for transfers between devices, sum_by_chip(): return lax.psum_scatter(pieces, chips, scatter_dimension=0, tiled=True)[0]  252 us
    reduce_scatter x2, waiting for transfers between devices, sum_by_axis(): running = lax.psum_scatter(running, axis, scatter_dimension=0, tiled=True)  139 us
    ppermute x4, starting transfers between devices, partner(): return lax.ppermute(value, axis, pairs)  52.8 us
    reduce_scatter x1, waiting for transfers between devices, sum_by_chip(): pieces = lax.psum_scatter(pieces, core, scatter_dimension=0, tiled=True)  37.4 us
  transfers between devices with their start and end apart: 8, of which 7 were waited for; matrix products, arithmetic and copies ran while one was open for 5% of the time, Pallas kernels for 0%

commit v1 on v0

v1 whole, which is shorter than its diff:
```python
import functools
import math

import jax
import jax.numpy as jnp
from jax import lax
from jax.experimental import pallas as pl
from jax.experimental.pallas import tpu as pltpu
from jax.sharding import Mesh
from jax.sharding import PartitionSpec as P

DP = ("y", "w", "c")
TENSOR = ("x", "v")
BF16 = jnp.bfloat16
F32 = jnp.float32


def dot(a, b, da, db):
    return lax.dot_general(a, b, (((da,), (db,)), ((), ())), preferred_element_type=F32)


def pack(a):
    rows = a.shape[0] // 2
    return jnp.concatenate([a[:rows], a[rows:]], axis=1)


def unpack(a):
    width = a.shape[1] // 2
    return jnp.concatenate([a[:, :width], a[:, width:]], axis=0)


def kernel(
    sizes,
    hidden_hbm,
    weight_hbm,
    query_hbm,
    key_hbm,
    out_hbm,
    grad_hbm,
    norm_ref,
    docs_ref,
    qgrad_ref,
    kgrad_ref,
    igrad_ref,
    wgrad_ref,
    hidden,
    weight,
    query,
    key_half,
    attn_out,
    grad,
    weight_rows,
    weight_cols,
    key_send,
    key_recv,
    val_send,
    val_recv,
    keys,
    values,
    probs,
    half_send,
    half_recv,
    kpart_send,
    kpart_recv,
    part_send,
    part_recv,
    plane_grads,
    plane_weights,
    out_send,
    out_recv,
    keep,
    core_send,
    core_recv,
    y_send,
    y_recv,
    w_send,
    w_recv,
    local_sem,
    hidden_sem,
    rows_sem,
    pair_send,
    pair_recv,
    x_sems,
    v_send,
    v_recv,
    part_ssem,
    part_rsem,
    chain_send,
    chain_recv,
    plane_sems,
    core_ssem,
    core_rsem,
    y_ssem,
    y_rsem,
    w_sems,
):
    NX, NY, NW, NC, NV = sizes
    T, D = hidden.shape
    half = key_half.shape[1]
    width = 2 * half
    heads = norm_ref.shape[1]
    scale = 1.0 / math.sqrt(width)
    NS = NX * NY * NC
    DS = D // NS
    DB = DS // 2
    RG = NW // 2
    R = half // RG
    TR = T // (NX * NV)
    TV = T // NV
    BD = D // (NY * NW * NC)
    x, y, w, c, v = (lax.axis_index(name) for name in ("x", "y", "w", "c", "v"))
    me = (x * NY + y) * NC + c
    member = v % 2
    lower = member == 0
    depth_half, row_group = w // RG, w % RG

    def plane(i):
        dx, dy, dc = i // (NY * NC), (i // NC) % NY, i % NC
        px, py, pc = (x + dx) % NX, (y + dy) % NY, (c + dc) % NC
        return {"x": px, "y": py, "c": pc}, (px * NY + py) * NC + pc

    position = v * NW + w
    after, before = (position + 1) % (NV * NW), (position + NV * NW - 1) % (NV * NW)
    up = {"v": after // NW, "w": after % NW}
    down = {"v": before // NW, "w": before % NW}
    pair = {"v": v + 1 - 2 * member}

    def remote(src, dst, send, recv, device):
        return pltpu.make_async_remote_copy(
            src_ref=src,
            dst_ref=dst,
            send_sem=send,
            recv_sem=recv,
            device_id=device,
            device_id_type=pl.DeviceIdType.MESH,
        )

    def wait_for(ref, sem):
        pltpu.make_async_copy(ref, ref, sem).wait()

    key_copy = pltpu.make_async_copy(key_hbm, key_half, local_sem.at[0])
    key_copy.start()
    row_copies = []
    for i in range(NX):
        start = ((i * NY + y) * NC + c) * DS + depth_half * DB
        row_copies.append(
            pltpu.make_async_copy(
                weight_hbm.at[pl.ds(pl.multiple_of(start, DB), DB)],
                weight_rows.at[i],
                rows_sem.at[i],
            )
        )
        row_copies[-1].start()
    weight_copy = pltpu.make_async_copy(weight_hbm, weight, local_sem.at[1])
    weight_copy.start()
    HC = D // 4
    hidden_copies = [
        pltpu.make_async_copy(
            hidden_hbm.at[:, pl.ds(i * HC, HC)], hidden.at[:, pl.ds(i * HC, HC)], hidden_sem.at[i]
        )
        for i in range(4)
    ]
    for copy in hidden_copies:
        copy.start()
    query_copy = pltpu.make_async_copy(query_hbm, query, local_sem.at[2])
    grad_copy = pltpu.make_async_copy(grad_hbm, grad, local_sem.at[3])
    out_copy = pltpu.make_async_copy(out_hbm, attn_out, local_sem.at[4])
    for copy in (query_copy, grad_copy, out_copy):
        copy.start()

    barrier = pltpu.get_barrier_semaphore()

    def greet(device):
        pl.semaphore_signal(
            barrier, inc=1, device_id=device, device_id_type=pl.DeviceIdType.MESH
        )

    greet({"v": (v + 1) % NV})
    greet({"v": (v + NV - 1) % NV})
    greet(up)
    greet(down)

    def greet_plane(i, carry):
        greet(plane(i)[0])
        return carry

    lax.fori_loop(1, NS, greet_plane, 0)

    def greet_line(i, carry):
        greet({"w": (w + i) % NW})
        return carry

    lax.fori_loop(1, NW, greet_line, 0)

    key_copy.wait()
    own_key = key_half[...].astype(F32)
    key_send[...] = pack(own_key).astype(BF16)
    for copy in row_copies:
        copy.wait()
    for i in range(0, NX, 2):
        both = jnp.concatenate(
            [weight_rows[i].astype(F32), weight_rows[i + 1].astype(F32)], axis=1
        ).T
        weight_cols[i] = both[:half].astype(BF16)
        weight_cols[i + 1] = both[half:].astype(BF16)

    weight_copy.wait()
    CK = 1024
    total = jnp.zeros((T, half), F32)
    for i in range(4):
        hidden_copies[i].wait()

        def add_values(k, acc, base=i * HC):
            at = pl.multiple_of(base + k * CK, CK)
            return acc + dot(hidden[:, pl.ds(at, CK)], weight[pl.ds(at, CK), :], 1, 0)

        total = lax.fori_loop(0, HC // CK, add_values, total)
    own_value = total.astype(BF16).astype(F32)
    val_send[...] = pack(own_value).astype(BF16)

    pl.semaphore_wait(barrier, 4 + (NS - 1) + (NW - 1))

    key_exchange = remote(key_send, key_recv, pair_send.at[0], pair_recv.at[0], pair)
    key_exchange.start()
    own_rows = pl.ds(pl.multiple_of(row_group * R, R), R)
    for i in range(1, NX):
        to = (x + i) % NX
        remote(
            weight_cols.at[to, own_rows],
            plane_weights.at[w, v, x],
            x_sems.at[0],
            x_sems.at[1],
            {"x": to},
        ).start()
    own_copy = pltpu.make_async_copy(
        weight_cols.at[x, own_rows], plane_weights.at[w, v, x], local_sem.at[5]
    )
    own_copy.start()
    value_exchange = remote(val_send, val_recv, pair_send.at[1], pair_recv.at[1], pair)
    value_exchange.start()

    own_copy.wait()
    wait_for(plane_weights.at[w, v, pl.ds(0, NX - 1)], x_sems.at[1])

    def weights_to(j):
        return remote(
            plane_weights.at[w, v],
            plane_weights.at[w, v],
            v_send.at[j],
            v_recv.at[j],
            {"v": (v + j) % NV},
        )

    weights_to(1).start()
    weights_to(3).start()

    query_copy.wait()
    grad_copy.wait()
    rows = lax.broadcasted_iota(jnp.int32, (T, T), 0)
    columns = lax.broadcasted_iota(jnp.int32, (T, T), 1)
    documents = jnp.broadcast_to(docs_ref[...].astype(F32), (T, T))
    allowed = (columns <= rows) & (documents == documents.T)

    key_exchange.wait_recv()
    other_key = unpack(key_recv[...].astype(F32))
    keys[...] = jnp.concatenate(
        [jnp.where(lower, own_key, other_key), jnp.where(lower, other_key, own_key)], axis=1
    ).astype(BF16)
    weights_to(2).start()

    value_part = jnp.zeros((T, width), F32)
    for h in range(heads):
        lanes = pl.ds(h * width, width)
        scores = dot(query[:, lanes], keys[...], 1, 1) * scale
        prob = jnp.where(allowed, jnp.exp(scores - norm_ref[:, h : h + 1]), 0.0)
        probs[h] = prob
        value_part = value_part + dot(prob.astype(BF16), grad[:, lanes], 0, 0)

    own_half = jnp.where(lower, value_part[:, :half], value_part[:, half:])
    other_half = jnp.where(lower, value_part[:, half:], value_part[:, :half])
    half_send[...] = pack(other_half).astype(BF16)
    half_exchange = remote(half_send, half_recv, pair_send.at[2], pair_recv.at[2], pair)
    half_exchange.start()
    by_token = value_part.reshape(NX, NV, TR, width)
    for i in range(NV):
        part_send[i] = by_token[:, i].reshape(TV, width).astype(BF16)

    def part_to(j):
        to = (v + j) % NV
        return remote(
            part_send.at[to], part_recv.at[v], part_ssem.at[j], part_rsem.at[j], {"v": to}
        )

    for j in (2, 1, 3):
        part_to(j).start()
    part_recv[v] = part_send[v]

    out_copy.wait()
    value_exchange.wait_recv()
    other_value = unpack(val_recv[...].astype(F32))
    values[...] = jnp.concatenate(
        [jnp.where(lower, own_value, other_value), jnp.where(lower, other_value, own_value)], axis=1
    ).astype(BF16)
    key_part = jnp.zeros((T, width), F32)
    for h in range(heads):
        lanes = pl.ds(h * width, width)
        head_grad = grad[:, lanes]
        row_dots = jnp.sum(
            head_grad.astype(F32) * attn_out[:, lanes].astype(F32), axis=1, keepdims=True
        )
        prob_grad = dot(head_grad, values[...], 1, 1)
        score_grad = (probs[h] * (prob_grad - row_dots) * scale).astype(BF16)
        qgrad_ref[:, lanes] = dot(score_grad, keys[...], 1, 0).astype(BF16)
        key_part = key_part + dot(score_grad, query[:, lanes], 0, 0)
    own_kpart = jnp.where(lower, key_part[:, :half], key_part[:, half:])
    other_kpart = jnp.where(lower, key_part[:, half:], key_part[:, :half])
    kpart_send[...] = pack(other_kpart).astype(BF16)
    kpart_exchange = remote(kpart_send, kpart_recv, pair_send.at[3], pair_recv.at[3], pair)
    kpart_exchange.start()

    half_exchange.wait_recv()
    value_grad = own_half + unpack(half_recv[...].astype(F32))
    value_grad_t = jnp.concatenate([value_grad, value_grad], axis=1).T[:half].astype(BF16)

    def core_copy(off):
        return remote(
            core_send.at[off],
            core_recv.at[off],
            core_ssem.at[off],
            core_rsem.at[off],
            {"c": 1 - c},
        )

    def make_blocks(off, carry):
        to_w = (w + off) % NW
        for j in range(NY):
            block = (((y + j) % NY) * NW + to_w) * NC
            own = pl.multiple_of((block + c) * BD, BD)
            other = pl.multiple_of((block + 1 - c) * BD, BD)
            core_send[off, j] = dot(value_grad_t, hidden[:, pl.ds(other, BD)], 1, 0).astype(BF16)
            keep[off, j] = dot(value_grad_t, hidden[:, pl.ds(own, BD)], 1, 0)
        core_copy(off).start()
        return carry

    lax.fori_loop(0, NW, make_blocks, 0)

    def send_y(off, carry):
        core_copy(off).wait_recv()
        for j in range(1, NY):
            y_send[off, j - 1] = (keep[off, j] + core_recv[off, j].astype(F32)).astype(BF16)
            remote(
                y_send.at[off, j - 1],
                y_recv.at[off, j - 1],
                y_ssem,
                y_rsem.at[off],
                {"y": (y + j) % NY},
            ).start()
        keep[off, 0] = keep[off, 0] + core_recv[off, 0].astype(F32)
        return carry

    lax.fori_loop(0, NW, send_y, 0)

    for j in (1, 3, 2):
        part_to(j).wait_recv()
    own_tokens = jnp.concatenate(
        [
            part_recv[2 * i].astype(F32) + part_recv[2 * i + 1].astype(F32)
            for i in range(NV // 2)
        ],
        axis=1,
    )
    plane_grads[me] = own_tokens.astype(BF16)

    def send_grads(i, carry):
        remote(
            plane_grads.at[me], plane_grads.at[me], plane_sems.at[0], plane_sems.at[1], plane(i)[0]
        ).start()
        return carry

    lax.fori_loop(1, NS, send_grads, 0)

    for j in (1, 3, 2):
        weights_to(j).wait_recv()
    UP, DOWN = NW // 2, (NW - 1) // 2

    def chain_up(k):
        block = plane_weights.at[(w + NW - k) % NW]
        return remote(block, block, chain_send.at[0, k], chain_recv.at[0, k], up)

    def chain_down(k):
        block = plane_weights.at[(w + k) % NW]
        return remote(block, block, chain_send.at[1, k], chain_recv.at[1, k], down)

    def send_w(off):
        wait_for(y_recv.at[off], y_rsem.at[off])
        summed = keep[off, 0]
        for j in range(NY - 1):
            summed = summed + y_recv[off, j].astype(F32)
        if off == 0:
            keep[0, 0] = summed
            return
        w_send[off - 1] = summed.astype(BF16)
        remote(
            w_send.at[off - 1],
            w_recv.at[off - 1],
            w_sems.at[0],
            w_sems.at[1],
            {"w": (w + off) % NW},
        ).start()

    chain_up(0).start()
    if DOWN:
        chain_down(0).start()
    pending = list(range(1, NW)) + [0]
    share = -(-NW // UP)
    for k in range(UP):
        for off in pending[k * share : (k + 1) * share]:
            send_w(off)
        chain_up(k).wait_recv()
        if k + 1 < UP:
            chain_up(k + 1).start()
        if k < DOWN:
            chain_down(k).wait_recv()
            if k + 1 < DOWN:
                chain_down(k + 1).start()

    wait_for(plane_grads.at[pl.ds(0, NS - 1)], plane_sems.at[1])
    NG = NY * NC
    pieces = []
    for d in range(2):
        acc = jnp.zeros((NG * TV, DB), F32)
        for i in range(NX):
            left = plane_grads[i * NG : (i + 1) * NG].reshape(NG * TV, NV * half)
            right = jnp.concatenate(
                [plane_weights[d * RG + g, k, i] for k in range(NV) for g in range(RG)], axis=0
            )
            acc = acc + dot(left, right, 1, 0)
        pieces.append(acc.reshape(NG, NX, TR, DB))
    for i in range(NX):
        out_send[i * NG : (i + 1) * NG] = jnp.concatenate(
            [pieces[0][:, i], pieces[1][:, i]], axis=1
        ).astype(BF16)

    def send_out(i, carry):
        device, slot = plane(i)
        remote(
            out_send.at[slot], out_recv.at[me], plane_sems.at[2], plane_sems.at[3], device
        ).start()
        return carry

    lax.fori_loop(1, NS, send_out, 0)
    out_recv[me] = out_send[me]

    kpart_exchange.wait_recv()
    kgrad_ref[...] = (own_kpart + unpack(kpart_recv[...].astype(F32))).astype(BF16)
    wait_for(w_recv, w_sems.at[1])
    summed = keep[0, 0]
    for off in range(NW - 1):
        summed = summed + w_recv[off].astype(F32)
    wgrad_ref[...] = summed
    wait_for(out_recv.at[pl.ds(0, NS - 1)], plane_sems.at[3])
    igrad_ref[...] = out_recv[...]

    for exchange in (key_exchange, value_exchange, half_exchange, kpart_exchange):
        exchange.wait_send()
    wait_for(plane_weights.at[w, v, pl.ds(0, NX - 1)], x_sems.at[0])
    for j in (1, 2, 3):
        weights_to(j).wait_send()
        part_to(j).wait_send()
    for k in range(UP):
        chain_up(k).wait_send()
    for k in range(DOWN):
        chain_down(k).wait_send()

    def core_sent(off, carry):
        core_copy(off).wait_send()
        return carry

    lax.fori_loop(0, NW, core_sent, 0)
    wait_for(y_send, y_ssem)
    wait_for(w_send, w_sems.at[0])
    wait_for(plane_grads.at[pl.ds(0, NS - 1)], plane_sems.at[0])
    wait_for(out_send.at[pl.ds(0, NS - 1)], plane_sems.at[2])


def per_device(
    sizes,
    hidden_in,
    value_weight,
    queries,
    key_rows,
    attention_out,
    output_grad,
    log_normalizer,
    document_ids,
):
    NX, NY, NW, NC, NV = sizes
    T, D = hidden_in.shape[1:]
    half = key_rows.shape[2]
    width = 2 * half
    heads = log_normalizer.shape[2]
    NS = NX * NY * NC
    DS = D // NS
    DB = DS // 2
    R = half // (NW // 2)
    TR = T // (NX * NV)
    TV = T // NV
    BD = D // (NY * NW * NC)
    packed = pltpu.VMEM((T // 2, 2 * half), BF16)
    dma = pltpu.SemaphoreType.DMA
    scratch = [
        pltpu.VMEM((T, D), BF16),
        pltpu.VMEM((D, half), BF16),
        pltpu.VMEM((T, heads * width), BF16),
        pltpu.VMEM((T, half), BF16),
        pltpu.VMEM((T, heads * width), BF16),
        pltpu.VMEM((T, heads * width), BF16),
        pltpu.VMEM((NX, DB, half), BF16),
        pltpu.VMEM((NX, half, DB), BF16),
        packed,
        packed,
        packed,
        packed,
        pltpu.VMEM((T, width), BF16),
        pltpu.VMEM((T, width), BF16),
        pltpu.VMEM((heads, T, T), F32),
        packed,
        packed,
        packed,
        packed,
        pltpu.VMEM((NV, TV, width), BF16),
        pltpu.VMEM((NV, TV, width), BF16),
        pltpu.VMEM((NS, TV, NV * half), BF16),
        pltpu.VMEM((NW, NV, NX, R, DB), BF16),
        pltpu.VMEM((NS, 2 * TR, DB), BF16),
        pltpu.VMEM((NS, 2 * TR, DB), BF16),
        pltpu.VMEM((NW, NY, half, BD), F32),
        pltpu.VMEM((NW, NY, half, BD), BF16),
        pltpu.VMEM((NW, NY, half, BD), BF16),
        pltpu.VMEM((NW, NY - 1, half, BD), BF16),
        pltpu.VMEM((NW, NY - 1, half, BD), BF16),
        pltpu.VMEM((NW - 1, half, BD), BF16),
        pltpu.VMEM((NW - 1, half, BD), BF16),
        dma((6,)),
        dma((4,)),
        dma((NX,)),
        dma((4,)),
        dma((4,)),
        dma((2,)),
        dma((NV,)),
        dma((NV,)),
        dma((NV,)),
        dma((NV,)),
        dma((2, NW)),
        dma((2, NW)),
        dma((4,)),
        dma((NW,)),
        dma((NW,)),
        dma,
        dma((NW,)),
        dma((2,)),
    ]
    anywhere = pl.BlockSpec(memory_space=pl.ANY)
    vmem = pl.BlockSpec(memory_space=pltpu.VMEM)
    query_grad, key_grad, input_blocks, weight_grad = pl.pallas_call(
        functools.partial(kernel, sizes),
        out_shape=(
            jax.ShapeDtypeStruct((T, heads * width), BF16),
            jax.ShapeDtypeStruct((T, half), BF16),
            jax.ShapeDtypeStruct((NS, 2 * TR, DB), BF16),
            jax.ShapeDtypeStruct((half, BD), F32),
        ),
        in_specs=[anywhere] * 6 + [vmem] * 2,
        out_specs=(vmem,) * 4,
        scratch_shapes=scratch,
        compiler_params=pltpu.CompilerParams(
            collective_id=0, has_side_effects=True, vmem_limit_bytes=48 * 1024 * 1024
        ),
    )(
        hidden_in[0],
        value_weight,
        queries[0],
        key_rows[0],
        attention_out[0],
        output_grad[0],
        log_normalizer[0],
        document_ids,
    )
    input_grad = (
        input_blocks.reshape(NS, 2, TR, DB).transpose(2, 0, 1, 3).reshape(1, TR, D)
    )
    return query_grad[None], key_grad[None], input_grad, weight_grad.T


def over(finer):
    sizes = tuple(finer.shape[name] for name in ("x", "y", "w", "c", "v"))
    return jax.shard_map(
        functools.partial(per_device, sizes),
        mesh=finer,
        in_specs=(
            P(DP, None, None),
            P(None, TENSOR),
            P(DP, None, TENSOR),
            P(DP, None, TENSOR),
            P(DP, None, TENSOR),
            P(DP, None, TENSOR),
            P(DP, None, TENSOR),
            P(DP, None),
        ),
        out_specs=(P(DP, None, TENSOR), P(DP, None, TENSOR), P(DP, TENSOR, None), P(DP, TENSOR)),
        check_vma=False,
    )


def solution(mesh):
    return over(Mesh(mesh.devices.reshape(4, 8, 2, 4, 4), DP + TENSOR))
```

time: 533 us -> 105 us (0.20)
  the two profiles are of different devices: /device:TPU:2 before, /device:TPU:1 now
where the time goes in v1:
time: 105 us
  Pallas kernels  92.8 us (88%)
  local copies, waits for them, and re-layouts  11.4 us (11%)
    pallas_call x1, Pallas kernels, per_device(): pl.pallas_call(functools.partial(kernel, sizes), out_shape=(jax.ShapeDtyp...  92.8 us
    unnamed x17, local copies, waits for them, and re-layouts  11.4 us

profile of v1, /device:TPU:1, one launch (start us, length us, event | category | flops | bytes accessed | tf_op | source)
XLA Modules:
  0.0 104.8 jit_solution(6464738224162094895)
XLA Ops:
  0.6 0.0 copy-start.4
  0.6 0.0 copy-start.3
  0.7 0.0 copy-start.2
  0.7 0.0 copy-start.1
  0.7 0.9 copy.12
  1.6 0.8 copy.13
  2.4 4.8 %copy.14.weight_hbm = bf16[16384,64]{1,0:T(8,128)(2,1)} copy(bf16[16384,64]{0,1:T(8,128)(2,1)} %param.9) | data formatting | bytes 4194304 | tf_op args[1]
  7.1 0.0 copy-done.4
  7.1 0.0 copy-done.3
  7.1 0.0 copy-done.2
  7.1 0.0 copy-done.1
  7.1 0.0 copy-start
  7.2 2.2 %copy-done = bf16[1,128,16384]{2,1,0:T(8,128)(2,1)S(1)} copy-done((bf16[1,128,16384]{2,1,0:T(8,128)(2,1)S(1)}, bf16[1,128,16384]{2,1,0:T(8,128)(2,1)}, u32[]{:S(2)}) %copy-start) | copy-done | bytes 4194328
  9.3 92.8 %shard_map.111 = (bf16[128,1024]{1,0:T(8,128)(2,1)S(1)}, bf16[128,64]{1,0:T(8,128)(2,1)S(1)}, bf16[32,16,256]{2,1,0:T(8,128)(2,1)S(1)}, f32[64,256]{1,0:T(8,128)S(1)}) custom-call(bf16[128,16384]{1,0:T(8,128)(2,1)S(1)} %bitcast.14, bf16[16384,64]{1,0:T(8,128)(2,1)} %copy.14.weight_hbm, bf16[128,1024]{1,0:T(8,128)(2,1)S(1)} %bitcast.16, ...), custom_call_target="tpu_custom_call" | custom-call | tf_op jit(solution)/shard_map/pallas_call | solution.py:565
  102.1 0.7 copy.15
  102.8 0.7 copy.19
  103.5 0.7 copy.20
  104.2 0.6 copy.21
Async XLA Ops:
  0.6 6.5 %copy-start.4 = (s32[1,128]{1,0:T(1,128)S(1)}, s32[1,128]{1,0:T(1,128)}, u32[]{:S(2)}) copy-start(s32[1,128]{1,0:T(1,128)} %docs_ref.1) | copy-start | bytes 1540
  0.6 6.5 %copy-start.3 = (bf16[1,128,1024]{2,1,0:T(8,128)(2,1)S(1)}, bf16[1,128,1024]{2,1,0:T(8,128)(2,1)}, u32[]{:S(2)}) copy-start(bf16[1,128,1024]{2,1,0:T(8,128)(2,1)} %param.13) | copy-start | bytes 786436
  0.7 6.5 %copy-start.2 = (bf16[1,128,1024]{2,1,0:T(8,128)(2,1)S(1)}, bf16[1,128,1024]{2,1,0:T(8,128)(2,1)}, u32[]{:S(2)}) copy-start(bf16[1,128,1024]{2,1,0:T(8,128)(2,1)} %param.12) | copy-start | bytes 786436
  0.7 6.5 %copy-start.1 = (bf16[1,128,1024]{2,1,0:T(8,128)(2,1)S(1)}, bf16[1,128,1024]{2,1,0:T(8,128)(2,1)}, u32[]{:S(2)}) copy-start(bf16[1,128,1024]{2,1,0:T(8,128)(2,1)} %param.10) | copy-start | bytes 786436
  7.1 2.2 %copy-start = (bf16[1,128,16384]{2,1,0:T(8,128)(2,1)S(1)}, bf16[1,128,16384]{2,1,0:T(8,128)(2,1)}, u32[]{:S(2)}) copy-start(bf16[1,128,16384]{2,1,0:T(8,128)(2,1)} %param.8) | copy-start | bytes 12582916

commit v2 on v1

v2 whole, which is shorter than its diff:
```python
import functools
import math

import jax
import jax.numpy as jnp
from jax import lax
from jax.experimental import pallas as pl
from jax.experimental.pallas import tpu as pltpu
from jax.sharding import Mesh
from jax.sharding import PartitionSpec as P

DP = ("y", "w", "c")
TENSOR = ("x", "v")
BF16 = jnp.bfloat16
F32 = jnp.float32


def dot(a, b, da, db):
    return lax.dot_general(a, b, (((da,), (db,)), ((), ())), preferred_element_type=F32)


def kernel(
    sizes,
    hidden_hbm,
    weight_hbm,
    query_hbm,
    key_hbm,
    out_hbm,
    grad_hbm,
    norm_hbm,
    docs_hbm,
    qgrad_ref,
    kgrad_ref,
    igrad_ref,
    wgrad_ref,
    norm_ref,
    docs_ref,
    hidden,
    weight,
    query,
    attn_out,
    grad,
    key_recv,
    val_recv,
    keys,
    values,
    probs,
    half_send,
    half_recv,
    kpart_send,
    kpart_recv,
    part_send,
    part_recv,
    plane_grads,
    plane_weights,
    out_send,
    out_recv,
    keep,
    core_send,
    core_recv,
    y_send,
    y_recv,
    w_send,
    w_recv,
    local_sem,
    hidden_sem,
    pair_send,
    pair_recv,
    x_sems,
    v_send,
    v_recv,
    part_ssem,
    part_rsem,
    chain_send,
    chain_recv,
    plane_sems,
    core_ssem,
    core_rsem,
    y_ssem,
    y_rsem,
    w_sems,
):
    NX, NY, NW, NC, NV = sizes
    T, D = hidden.shape
    half = weight.shape[0]
    width = 2 * half
    heads = norm_ref.shape[0]
    scale = 1.0 / math.sqrt(width)
    NS = NX * NY * NC
    DS = D // NS
    DB = DS // 2
    RG = NW // 2
    R = half // RG
    TR = T // (NX * NV)
    TV = T // NV
    BD = D // (NY * NW * NC)
    x, y, w, c, v = (lax.axis_index(name) for name in ("x", "y", "w", "c", "v"))
    me = (x * NY + y) * NC + c
    member = v % 2
    lower = member == 0
    depth_half, row_group = w // RG, w % RG

    def plane(i):
        dx, dy, dc = i // (NY * NC), (i // NC) % NY, i % NC
        px, py, pc = (x + dx) % NX, (y + dy) % NY, (c + dc) % NC
        return {"x": px, "y": py, "c": pc}, (px * NY + py) * NC + pc

    position = v * NW + w
    after, before = (position + 1) % (NV * NW), (position + NV * NW - 1) % (NV * NW)
    up = {"v": after // NW, "w": after % NW}
    down = {"v": before // NW, "w": before % NW}
    pair = {"v": v + 1 - 2 * member}

    def remote(src, dst, send, recv, device):
        return pltpu.make_async_remote_copy(
            src_ref=src,
            dst_ref=dst,
            send_sem=send,
            recv_sem=recv,
            device_id=device,
            device_id_type=pl.DeviceIdType.MESH,
        )

    def wait_for(ref, sem):
        pltpu.make_async_copy(ref, ref, sem).wait()

    own_half_rows = pl.ds(pl.multiple_of(member * half, half), half)
    other_half_rows = pl.ds(pl.multiple_of((1 - member) * half, half), half)
    key_copy = pltpu.make_async_copy(key_hbm, keys.at[own_half_rows], local_sem.at[0])
    key_copy.start()
    weight_copy = pltpu.make_async_copy(weight_hbm, weight, local_sem.at[1])
    weight_copy.start()
    HC = D // 4
    hidden_copies = [
        pltpu.make_async_copy(
            hidden_hbm.at[:, pl.ds(i * HC, HC)], hidden.at[:, pl.ds(i * HC, HC)], hidden_sem.at[i]
        )
        for i in range(4)
    ]
    for copy in hidden_copies:
        copy.start()
    query_copy = pltpu.make_async_copy(query_hbm, query, local_sem.at[2])
    grad_copy = pltpu.make_async_copy(grad_hbm, grad, local_sem.at[3])
    out_copy = pltpu.make_async_copy(out_hbm, attn_out, local_sem.at[4])
    norm_copy = pltpu.make_async_copy(norm_hbm, norm_ref, local_sem.at[6])
    docs_copy = pltpu.make_async_copy(docs_hbm, docs_ref, local_sem.at[7])
    for copy in (norm_copy, docs_copy, query_copy, grad_copy, out_copy):
        copy.start()

    barrier = pltpu.get_barrier_semaphore()

    def greet(device):
        pl.semaphore_signal(
            barrier, inc=1, device_id=device, device_id_type=pl.DeviceIdType.MESH
        )

    greet({"v": (v + 1) % NV})
    greet({"v": (v + NV - 1) % NV})
    greet(up)
    greet(down)

    def greet_plane(i, carry):
        greet(plane(i)[0])
        return carry

    lax.fori_loop(1, NS, greet_plane, 0)

    def greet_line(i, carry):
        greet({"w": (w + i) % NW})
        return carry

    lax.fori_loop(1, NW, greet_line, 0)

    weight_copy.wait()
    CK = 1024
    total = jnp.zeros((half, T), F32)
    for i in range(4):
        hidden_copies[i].wait()

        def add_values(k, acc, base=i * HC):
            at = pl.ds(pl.multiple_of(base + k * CK, CK), CK)
            return acc + dot(weight[:, at], hidden[:, at], 1, 1)

        total = lax.fori_loop(0, HC // CK, add_values, total)
    values[own_half_rows, :] = total.astype(BF16)
    norm_copy.wait()
    docs_copy.wait()
    norm = jnp.concatenate([norm_ref[...]] * (T // heads), axis=0).T
    rows = lax.broadcasted_iota(jnp.int32, (T, T), 0)
    columns = lax.broadcasted_iota(jnp.int32, (T, T), 1)
    documents = jnp.broadcast_to(docs_ref[...].astype(F32), (T, T))
    allowed = (columns <= rows) & (documents == documents.T)
    key_copy.wait()

    pl.semaphore_wait(barrier, 4 + (NS - 1) + (NW - 1))

    key_exchange = remote(keys.at[own_half_rows], key_recv, pair_send.at[0], pair_recv.at[0], pair)
    key_exchange.start()
    own_rows = pl.ds(pl.multiple_of(row_group * R, R), R)

    def weight_piece(to):
        start = ((to * NY + y) * NC + c) * DS + depth_half * DB
        return weight.at[own_rows, pl.ds(pl.multiple_of(start, DB), DB)]

    for i in range(1, NX):
        to = (x + i) % NX
        remote(
            weight_piece(to),
            plane_weights.at[w, v, x],
            x_sems.at[0],
            x_sems.at[1],
            {"x": to},
        ).start()
    own_copy = pltpu.make_async_copy(
        weight_piece(x), plane_weights.at[w, v, x], local_sem.at[5]
    )
    own_copy.start()
    value_exchange = remote(values.at[own_half_rows], val_recv, pair_send.at[1], pair_recv.at[1], pair)

    own_copy.wait()
    wait_for(plane_weights.at[w, v, pl.ds(0, NX - 1)], x_sems.at[1])

    def weights_to(j):
        block = plane_weights.at[w, v]
        return remote(block, block, v_send.at[j], v_recv.at[j], {"v": (v + j) % NV})

    def weights_on(j):
        first = 0 if j == 1 else NX // 2
        block = plane_weights.at[w, (v + NV - j) % NV, pl.ds(first, NX // 2)]
        return remote(block, block, v_send.at[j - 1], v_recv.at[j - 1], {"v": (v + j) % NV})

    weights_to(1).start()
    weights_to(3).start()

    query_copy.wait()
    grad_copy.wait()
    key_exchange.wait_recv()
    keys[other_half_rows, :] = key_recv[...]

    value_part = jnp.zeros((width, T), F32)
    for h in range(heads):
        lanes = pl.ds(h * width, width)
        scores = dot(query[:, lanes], keys[...], 1, 0) * scale
        prob = jnp.where(allowed, jnp.exp(scores - norm[:, h : h + 1]), 0.0)
        probs[h] = prob
        value_part = value_part + dot(grad[:, lanes], prob.astype(BF16), 0, 0)

    own_half = jnp.where(lower, value_part[:half], value_part[half:])
    half_send[...] = jnp.where(lower, value_part[half:], value_part[:half]).astype(BF16)
    half_exchange = remote(half_send, half_recv, pair_send.at[2], pair_recv.at[2], pair)
    half_exchange.start()
    by_token = value_part.T.reshape(NX, NV, TR, width)
    for i in range(NV):
        part_send[i] = by_token[:, i].reshape(TV, width).astype(BF16)

    def part_to(j):
        to = (v + j) % NV
        return remote(
            part_send.at[to], part_recv.at[v], part_ssem.at[j], part_rsem.at[j], {"v": to}
        )

    for j in (2, 1, 3):
        part_to(j).start()
    part_recv[v] = part_send[v]
    value_exchange.start()

    weights_to(1).wait_recv()
    weights_on(1).start()
    weights_to(3).wait_recv()
    weights_on(3).start()

    half_exchange.wait_recv()
    value_grad_t = (own_half + half_recv[...].astype(F32)).astype(BF16)

    def core_copy(off):
        return remote(
            core_send.at[off],
            core_recv.at[off],
            core_ssem.at[off],
            core_rsem.at[off],
            {"c": 1 - c},
        )

    def make_blocks(off, carry):
        to_w = (w + off) % NW
        for j in range(NY):
            block = (((y + j) % NY) * NW + to_w) * NC
            own = pl.multiple_of((block + c) * BD, BD)
            other = pl.multiple_of((block + 1 - c) * BD, BD)
            core_send[off, j] = dot(value_grad_t, hidden[:, pl.ds(other, BD)], 1, 0).astype(BF16)
            keep[off, j] = dot(value_grad_t, hidden[:, pl.ds(own, BD)], 1, 0)
        core_copy(off).start()
        return carry

    lax.fori_loop(0, NW, make_blocks, 0)

    def send_y(off, carry):
        core_copy(off).wait_recv()
        for j in range(1, NY):
            y_send[off, j - 1] = (keep[off, j] + core_recv[off, j].astype(F32)).astype(BF16)
            remote(
                y_send.at[off, j - 1],
                y_recv.at[off, j - 1],
                y_ssem,
                y_rsem.at[off],
                {"y": (y + j) % NY},
            ).start()
        keep[off, 0] = keep[off, 0] + core_recv[off, 0].astype(F32)
        return carry

    lax.fori_loop(0, NW // 2, send_y, 0)

    weights_on(1).wait_recv()
    weights_on(3).wait_recv()
    UP, DOWN = NW // 2, (NW - 1) // 2
    HV = NV // 2

    def chain_up(k, part):
        block = plane_weights.at[(w + NW - k) % NW, pl.ds(part * HV, HV)]
        return remote(block, block, chain_send.at[0, k, part], chain_recv.at[0, k, part], up)

    def chain_down(k, part):
        block = plane_weights.at[(w + k) % NW, pl.ds(part * HV, HV)]
        return remote(block, block, chain_send.at[1, k, part], chain_recv.at[1, k, part], down)

    for part in range(2):
        chain_up(0, part).start()
        if DOWN:
            chain_down(0, part).start()

    def pass_on(k):
        for part in range(2):
            chain_up(k, part).wait_recv()
            if k + 1 < UP:
                chain_up(k + 1, part).start()
            if k < DOWN:
                chain_down(k, part).wait_recv()
                if k + 1 < DOWN:
                    chain_down(k + 1, part).start()

    for j in (1, 3, 2):
        part_to(j).wait_recv()
    own_tokens = jnp.concatenate(
        [
            part_recv[2 * i].astype(F32) + part_recv[2 * i + 1].astype(F32)
            for i in range(NV // 2)
        ],
        axis=1,
    )
    plane_grads[me] = own_tokens.astype(BF16)

    def send_grads(i, carry):
        remote(
            plane_grads.at[me], plane_grads.at[me], plane_sems.at[0], plane_sems.at[1], plane(i)[0]
        ).start()
        return carry

    lax.fori_loop(1, NS, send_grads, 0)
    lax.fori_loop(NW // 2, NW, send_y, 0)
    pass_on(0)

    out_copy.wait()
    value_exchange.wait_recv()
    values[other_half_rows, :] = val_recv[...]
    key_part = jnp.zeros((width, T), F32)
    for h in range(heads):
        lanes = pl.ds(h * width, width)
        head_grad = grad[:, lanes]
        row_dots = jnp.sum(
            head_grad.astype(F32) * attn_out[:, lanes].astype(F32), axis=1, keepdims=True
        )
        prob_grad = dot(head_grad, values[...], 1, 0)
        score_grad = (probs[h] * (prob_grad - row_dots) * scale).astype(BF16)
        qgrad_ref[:, lanes] = dot(score_grad, keys[...], 1, 1).astype(BF16)
        key_part = key_part + dot(query[:, lanes], score_grad, 0, 0)
    own_kpart = jnp.where(lower, key_part[:half], key_part[half:])
    kpart_send[...] = jnp.where(lower, key_part[half:], key_part[:half]).astype(BF16)
    kpart_exchange = remote(kpart_send, kpart_recv, pair_send.at[3], pair_recv.at[3], pair)
    kpart_exchange.start()
    if UP > 1:
        pass_on(1)

    def send_w(off):
        wait_for(y_recv.at[off], y_rsem.at[off])
        summed = keep[off, 0]
        for j in range(NY - 1):
            summed = summed + y_recv[off, j].astype(F32)
        if off == 0:
            keep[0, 0] = summed
            return
        w_send[off - 1] = summed.astype(BF16)
        remote(
            w_send.at[off - 1],
            w_recv.at[off - 1],
            w_sems.at[0],
            w_sems.at[1],
            {"w": (w + off) % NW},
        ).start()

    pending = list(range(1, NW)) + [0]
    share = -(-NW // UP)
    for k in range(UP):
        for off in pending[k * share : (k + 1) * share]:
            send_w(off)
        if k > 1:
            pass_on(k)

    wait_for(plane_grads.at[pl.ds(0, NS - 1)], plane_sems.at[1])
    NG = NY * NC
    pieces = []
    for d in range(2):
        acc = jnp.zeros((NG * TV, DB), F32)
        for i in range(NX):
            left = plane_grads[i * NG : (i + 1) * NG].reshape(NG * TV, NV * half)
            right = jnp.concatenate(
                [plane_weights[d * RG + g, k, i] for k in range(NV) for g in range(RG)], axis=0
            )
            acc = acc + dot(left, right, 1, 0)
        pieces.append(acc.reshape(NG, NX, TR, DB))
    for i in range(NX):
        out_send[i * NG : (i + 1) * NG] = jnp.concatenate(
            [pieces[0][:, i], pieces[1][:, i]], axis=1
        ).astype(BF16)

    def send_out(i, carry):
        device, slot = plane(i)
        remote(
            out_send.at[slot], out_recv.at[me], plane_sems.at[2], plane_sems.at[3], device
        ).start()
        return carry

    lax.fori_loop(1, NS, send_out, 0)
    out_recv[me] = out_send[me]

    kpart_exchange.wait_recv()
    kgrad_ref[...] = (own_kpart + kpart_recv[...].astype(F32)).astype(BF16)
    wait_for(w_recv, w_sems.at[1])
    summed = keep[0, 0]
    for off in range(NW - 1):
        summed = summed + w_recv[off].astype(F32)
    wgrad_ref[...] = summed
    wait_for(out_recv.at[pl.ds(0, NS - 1)], plane_sems.at[3])
    igrad_ref[...] = out_recv[...]

    for exchange in (key_exchange, value_exchange, half_exchange, kpart_exchange):
        exchange.wait_send()
    wait_for(plane_weights.at[w, v, pl.ds(0, NX - 1)], x_sems.at[0])
    for j in (1, 3):
        weights_to(j).wait_send()
        weights_on(j).wait_send()
    for j in (1, 2, 3):
        part_to(j).wait_send()
    for part in range(2):
        for k in range(UP):
            chain_up(k, part).wait_send()
        for k in range(DOWN):
            chain_down(k, part).wait_send()

    def core_sent(off, carry):
        core_copy(off).wait_send()
        return carry

    lax.fori_loop(0, NW, core_sent, 0)
    wait_for(y_send, y_ssem)
    wait_for(w_send, w_sems.at[0])
    wait_for(plane_grads.at[pl.ds(0, NS - 1)], plane_sems.at[0])
    wait_for(out_send.at[pl.ds(0, NS - 1)], plane_sems.at[2])


def hand_over(*refs):
    sems = refs[-1]
    copies = [
        pltpu.make_async_copy(source, target, sems.at[i])
        for i, (source, target) in enumerate(zip(refs[:4], refs[4:8]))
    ]
    for copy in copies:
        copy.start()
    for copy in copies:
        copy.wait()


def per_device(
    sizes,
    hidden_in,
    value_weight,
    queries,
    key_rows,
    attention_out,
    output_grad,
    log_normalizer,
    document_ids,
):
    NX, NY, NW, NC, NV = sizes
    T, D = hidden_in.shape[1:]
    half = key_rows.shape[2]
    width = 2 * half
    heads = log_normalizer.shape[2]
    NS = NX * NY * NC
    DS = D // NS
    DB = DS // 2
    R = half // (NW // 2)
    TR = T // (NX * NV)
    TV = T // NV
    BD = D // (NY * NW * NC)
    half_block = pltpu.VMEM((half, T), BF16)
    dma = pltpu.SemaphoreType.DMA
    scratch = [
        pltpu.VMEM((heads, T), F32),
        pltpu.VMEM((1, T), jnp.int32),
        pltpu.VMEM((T, D), BF16),
        pltpu.VMEM((half, D), BF16),
        pltpu.VMEM((T, heads * width), BF16),
        pltpu.VMEM((T, heads * width), BF16),
        pltpu.VMEM((T, heads * width), BF16),
        half_block,
        half_block,
        pltpu.VMEM((width, T), BF16),
        pltpu.VMEM((width, T), BF16),
        pltpu.VMEM((heads, T, T), F32),
        half_block,
        half_block,
        half_block,
        half_block,
        pltpu.VMEM((NV, TV, width), BF16),
        pltpu.VMEM((NV, TV, width), BF16),
        pltpu.VMEM((NS, TV, NV * half), BF16),
        pltpu.VMEM((NW, NV, NX, R, DB), BF16),
        pltpu.VMEM((NS, 2 * TR, DB), BF16),
        pltpu.VMEM((NS, 2 * TR, DB), BF16),
        pltpu.VMEM((NW, NY, half, BD), F32),
        pltpu.VMEM((NW, NY, half, BD), BF16),
        pltpu.VMEM((NW, NY, half, BD), BF16),
        pltpu.VMEM((NW, NY - 1, half, BD), BF16),
        pltpu.VMEM((NW, NY - 1, half, BD), BF16),
        pltpu.VMEM((NW - 1, half, BD), BF16),
        pltpu.VMEM((NW - 1, half, BD), BF16),
        dma((8,)),
        dma((4,)),
        dma((4,)),
        dma((4,)),
        dma((2,)),
        dma((NV,)),
        dma((NV,)),
        dma((NV,)),
        dma((NV,)),
        dma((2, NW, 2)),
        dma((2, NW, 2)),
        dma((4,)),
        dma((NW,)),
        dma((NW,)),
        dma,
        dma((NW,)),
        dma((2,)),
    ]
    anywhere = pl.BlockSpec(memory_space=pltpu.HBM)
    vmem = pl.BlockSpec(memory_space=pltpu.VMEM)
    results = pl.pallas_call(
        functools.partial(kernel, sizes),
        out_shape=(
            jax.ShapeDtypeStruct((T, heads * width), BF16),
            jax.ShapeDtypeStruct((half, T), BF16),
            jax.ShapeDtypeStruct((NS, 2 * TR, DB), BF16),
            jax.ShapeDtypeStruct((half, BD), F32),
        ),
        in_specs=[anywhere] * 8,
        out_specs=(vmem,) * 4,
        scratch_shapes=scratch,
        compiler_params=pltpu.CompilerParams(
            collective_id=0, has_side_effects=True, vmem_limit_bytes=48 * 1024 * 1024
        ),
    )(
        *(
            pltpu.with_memory_space_constraint(array, pltpu.HBM)
            for array in (
                hidden_in[0],
                value_weight.T,
                queries[0],
                key_rows[0].T,
                attention_out[0],
                output_grad[0],
                log_normalizer[0].T,
                document_ids,
            )
        )
    )
    query_grad, key_grad, input_blocks, weight_grad = pl.pallas_call(
        hand_over,
        out_shape=tuple(jax.ShapeDtypeStruct(r.shape, r.dtype) for r in results),
        in_specs=(vmem,) * 4,
        out_specs=(anywhere,) * 4,
        scratch_shapes=[dma((4,))],
        compiler_params=pltpu.CompilerParams(vmem_limit_bytes=8 * 1024 * 1024),
    )(*results)
    input_grad = (
        input_blocks.reshape(NS, 2, TR, DB).transpose(2, 0, 1, 3).reshape(1, TR, D)
    )
    return query_grad[None], key_grad.T[None], input_grad, weight_grad.T


def over(finer):
    sizes = tuple(finer.shape[name] for name in ("x", "y", "w", "c", "v"))
    return jax.shard_map(
        functools.partial(per_device, sizes),
        mesh=finer,
        in_specs=(
            P(DP, None, None),
            P(None, TENSOR),
            P(DP, None, TENSOR),
            P(DP, None, TENSOR),
            P(DP, None, TENSOR),
            P(DP, None, TENSOR),
            P(DP, None, TENSOR),
            P(DP, None),
        ),
        out_specs=(P(DP, None, TENSOR), P(DP, None, TENSOR), P(DP, TENSOR, None), P(DP, TENSOR)),
        check_vma=False,
    )


def solution(mesh):
    return over(Mesh(mesh.devices.reshape(4, 8, 2, 4, 4), DP + TENSOR))
```

time: 105 us -> 86.2 us (0.82)
  local copies, waits for them, and re-layouts: 11.4 us -> 0 us
  Pallas kernels: 92.8 us -> 85.4 us
    unnamed x17 -> x0, local copies, waits for them, and re-layouts: 11.4 us -> none
    pallas_call x1, Pallas kernels: 92.8 us -> 84.6 us  [per_device(): pl.pallas_call(functools.partial(kernel, sizes), out_shape=(jax.ShapeDtyp...]
where the time goes in v2:
time: 86.2 us; the launch traced here: 86.1 us
  Pallas kernels  85.4 us (99%)
    pallas_call x1, Pallas kernels, per_device(): pl.pallas_call(functools.partial(kernel, sizes), out_shape=(jax.ShapeDtyp...  84.6 us

profile of v2, /device:TPU:1, one launch (start us, length us, event | category | flops | bytes accessed | tf_op | source)
XLA Modules:
  0.0 86.1 jit_solution(8980900677870065759)
XLA Ops:
  0.6 84.6 %shard_map.111 = (bf16[128,1024]{1,0:T(8,128)(2,1)S(1)}, bf16[64,128]{1,0:T(8,128)(2,1)S(1)}, bf16[32,16,256]{2,1,0:T(8,128)(2,1)S(1)}, f32[64,256]{1,0:T(8,128)S(1)}) custom-call(bf16[128,16384]{1,0:T(8,128)(2,1)} %bitcast.21, bf16[64,16384]{1,0:T(8,128)(2,1)} %bitcast.22, bf16[128,1024]{1,0:T(8,128)(2,1)} %bitcast.23, bf16[64,128]{1,0:T(8,128)(2,1)} %bitcast.26, ...), custom_call_target="tpu_custom_call" | custom-call | tf_op jit(solution)/shard_map/pallas_call | solution.py:557
  85.2 0.8 shard_map.112

commit v3 on v2

--- a/solution.py
+++ b/solution.py
@@ -37,6 +37,7 @@
     docs_ref,
     hidden,
     weight,
+    weight_send,
     query,
     attn_out,
     grad,
@@ -58,12 +59,15 @@
     keep,
     core_send,
     core_recv,
+    far_send,
+    far_recv,
     y_send,
     y_recv,
     w_send,
     w_recv,
     local_sem,
     hidden_sem,
+    piece_sem,
     pair_send,
     pair_recv,
     x_sems,
@@ -76,9 +80,12 @@
     plane_sems,
     core_ssem,
     core_rsem,
+    far_ssem,
+    far_rsem,
     y_ssem,
     y_rsem,
-    w_sems,
+    w_ssem,
+    w_rsem,
 ):
     NX, NY, NW, NC, NV = sizes
     T, D = hidden.shape
@@ -124,12 +131,38 @@
     def wait_for(ref, sem):
         pltpu.make_async_copy(ref, ref, sem).wait()
 
+    barrier = pltpu.get_barrier_semaphore()
+
+    def greet(device):
+        pl.semaphore_signal(
+            barrier, inc=1, device_id=device, device_id_type=pl.DeviceIdType.MESH
+        )
+
+    greet({"v": (v + 1) % NV})
+    greet({"v": (v + NV - 1) % NV})
+
     own_half_rows = pl.ds(pl.multiple_of(member * half, half), half)
     other_half_rows = pl.ds(pl.multiple_of((1 - member) * half, half), half)
     key_copy = pltpu.make_async_copy(key_hbm, keys.at[own_half_rows], local_sem.at[0])
     key_copy.start()
+    own_rows = pl.ds(pl.multiple_of(row_group * R, R), R)
+    piece_copies = []
+    for i in range(NX):
+        to = (x + i) % NX
+        start = ((to * NY + y) * NC + c) * DS + depth_half * DB
+        piece_copies.append(
+            pltpu.make_async_copy(
+                weight_hbm.at[own_rows, pl.ds(pl.multiple_of(start, DB), DB)],
+                weight_send.at[i] if i else plane_weights.at[w, v, x],
+                piece_sem.at[i],
+            )
+        )
+        piece_copies[i].start()
+    norm_copy = pltpu.make_async_copy(norm_hbm, norm_ref, local_sem.at[5])
+    docs_copy = pltpu.make_async_copy(docs_hbm, docs_ref, local_sem.at[6])
     weight_copy = pltpu.make_async_copy(weight_hbm, weight, local_sem.at[1])
-    weight_copy.start()
+    for copy in (norm_copy, docs_copy, weight_copy):
+        copy.start()
     HC = D // 4
     hidden_copies = [
         pltpu.make_async_copy(
@@ -137,25 +170,12 @@
         )
         for i in range(4)
     ]
-    for copy in hidden_copies:
-        copy.start()
     query_copy = pltpu.make_async_copy(query_hbm, query, local_sem.at[2])
     grad_copy = pltpu.make_async_copy(grad_hbm, grad, local_sem.at[3])
     out_copy = pltpu.make_async_copy(out_hbm, attn_out, local_sem.at[4])
-    norm_copy = pltpu.make_async_copy(norm_hbm, norm_ref, local_sem.at[6])
-    docs_copy = pltpu.make_async_copy(docs_hbm, docs_ref, local_sem.at[7])
-    for copy in (norm_copy, docs_copy, query_copy, grad_copy, out_copy):
+    for copy in (*hidden_copies, query_copy, grad_copy, out_copy):
         copy.start()
 
-    barrier = pltpu.get_barrier_semaphore()
-
-    def greet(device):
-        pl.semaphore_signal(
-            barrier, inc=1, device_id=device, device_id_type=pl.DeviceIdType.MESH
-        )
-
-    greet({"v": (v + 1) % NV})
-    greet({"v": (v + NV - 1) % NV})
     greet(up)
     greet(down)
 
@@ -171,18 +191,24 @@
 
     lax.fori_loop(1, NW, greet_line, 0)
 
+    key_copy.wait()
+    for copy in piece_copies:
+        copy.wait()
+    pl.semaphore_wait(barrier, 4 + (NS - 1) + (NW - 1))
+
+    key_exchange = remote(keys.at[own_half_rows], key_recv, pair_send.at[0], pair_recv.at[0], pair)
+    key_exchange.start()
+    for i in range(1, NX):
+        remote(
+            weight_send.at[i],
+            plane_weights.at[w, v, x],
+            x_sems.at[0],
+            x_sems.at[1],
+            {"x": (x + i) % NX},
+        ).start()
+
     weight_copy.wait()
-    CK = 1024
-    total = jnp.zeros((half, T), F32)
-    for i in range(4):
-        hidden_copies[i].wait()
-
-        def add_values(k, acc, base=i * HC):
-            at = pl.ds(pl.multiple_of(base + k * CK, CK), CK)
-            return acc + dot(weight[:, at], hidden[:, at], 1, 1)
-
-        total = lax.fori_loop(0, HC // CK, add_values, total)
-    values[own_half_rows, :] = total.astype(BF16)
+
     norm_copy.wait()
     docs_copy.wait()
     norm = jnp.concatenate([norm_ref[...]] * (T // heads), axis=0).T
@@ -190,34 +216,17 @@
     columns = lax.broadcasted_iota(jnp.int32, (T, T), 1)
     documents = jnp.broadcast_to(docs_ref[...].astype(F32), (T, T))
     allowed = (columns <= rows) & (documents == documents.T)
-    key_copy.wait()
-
-    pl.semaphore_wait(barrier, 4 + (NS - 1) + (NW - 1))
-
-    key_exchange = remote(keys.at[own_half_rows], key_recv, pair_send.at[0], pair_recv.at[0], pair)
-    key_exchange.start()
-    own_rows = pl.ds(pl.multiple_of(row_group * R, R), R)
-
-    def weight_piece(to):
-        start = ((to * NY + y) * NC + c) * DS + depth_half * DB
-        return weight.at[own_rows, pl.ds(pl.multiple_of(start, DB), DB)]
-
-    for i in range(1, NX):
-        to = (x + i) % NX
-        remote(
-            weight_piece(to),
-            plane_weights.at[w, v, x],
-            x_sems.at[0],
-            x_sems.at[1],
-            {"x": to},
-        ).start()
-    own_copy = pltpu.make_async_copy(
-        weight_piece(x), plane_weights.at[w, v, x], local_sem.at[5]
-    )
-    own_copy.start()
-    value_exchange = remote(values.at[own_half_rows], val_recv, pair_send.at[1], pair_recv.at[1], pair)
-
-    own_copy.wait()
+    CK = 1024
+
+    def add_values(k, acc):
+        at = pl.ds(pl.multiple_of(k * CK, CK), CK)
+        return acc + dot(weight[:, at], hidden[:, at], 1, 1)
+
+    total = jnp.zeros((half, T), F32)
+    for i in range(2):
+        hidden_copies[i].wait()
+        total = lax.fori_loop(i * HC // CK, (i + 1) * HC // CK, add_values, total)
+
     wait_for(plane_weights.at[w, v, pl.ds(0, NX - 1)], x_sems.at[1])
 
     def weights_to(j):
@@ -231,6 +240,11 @@
 
     weights_to(1).start()
     weights_to(3).start()
+
+    for i in range(2, 4):
+        hidden_copies[i].wait()
+        total = lax.fori_loop(i * HC // CK, (i + 1) * HC // CK, add_values, total)
+    values[own_half_rows, :] = total.astype(BF16)
 
     query_copy.wait()
     grad_copy.wait()
@@ -262,12 +276,52 @@
     for j in (2, 1, 3):
         part_to(j).start()
     part_recv[v] = part_send[v]
-    value_exchange.start()
+    def spread(i, carry):
+        residue = (w + i) % NW
+        at = pl.ds(pl.multiple_of(residue % RG * R, R), R)
+        for k in range(NX):
+            to = (x + k) % NX
+            start = ((to * NY + y) * NC + c) * DS + residue // RG * DB
+            source = weight.at[at, pl.ds(pl.multiple_of(start, DB), DB)]
+            target = plane_weights.at[residue, v, x]
+            if k:
+                remote(source, target, x_sems.at[2], x_sems.at[3], {"x": to}).start()
+            else:
+                pltpu.make_async_copy(source, target, local_sem.at[7]).start()
+        return carry
+
+    lax.fori_loop(1, NW, spread, 0)
 
     weights_to(1).wait_recv()
     weights_on(1).start()
     weights_to(3).wait_recv()
     weights_on(3).start()
+
+    UP, DOWN = NW // 2, (NW - 1) // 2
+    PIECES = ((3, 2, 1), (1, 2, 3))
+
+    def chain(way, k, q):
+        origin = (position + (NV * NW - k if way == 0 else k)) % (NV * NW)
+        to = (up, down)[way]
+        block = plane_weights.at[origin % NW, (to["v"] + q) % NV]
+        return remote(block, block, chain_send.at[way, k, q], chain_recv.at[way, k, q], to)
+
+    def start_chain():
+        for qs in zip(*PIECES):
+            for way, steps in enumerate((UP, DOWN)):
+                if steps:
+                    chain(way, 0, qs[way]).start()
+
+    def pass_on(k):
+        for qs in zip(*PIECES):
+            for way, steps in enumerate((UP, DOWN)):
+                if k < steps:
+                    chain(way, k, qs[way]).wait_recv()
+                if k + 1 < steps:
+                    chain(way, k + 1, qs[way]).start()
+
+    value_exchange = remote(values.at[own_half_rows], val_recv, pair_send.at[1], pair_recv.at[1], pair)
+    value_exchange.start()
 
     half_exchange.wait_recv()
     value_grad_t = (own_half + half_recv[...].astype(F32)).astype(BF16)
@@ -294,49 +348,81 @@
 
     lax.fori_loop(0, NW, make_blocks, 0)
 
+    quarter = half // 2
+
+    def part_sum(off, j):
+        return keep[off, j] + core_recv[off, j].astype(F32)
+
+    def far_copy(off, way):
+        at = pl.ds(way * quarter, quarter)
+        return remote(
+            far_send.at[off, at],
+            far_recv.at[off, at],
+            far_ssem,
+            far_rsem.at[off],
+            {"y": (y + (1, NY - 1)[way]) % NY},
+        )
+
+    def y_copy(off, way):
+        return remote(
+            y_send.at[off, way],
+            y_recv.at[off, way],
+            y_ssem,
+            y_rsem.at[off],
+            {"y": (y + (1, NY - 1)[way]) % NY},
+        )
+
+    def send_far(off, carry):
+        core_copy(off).wait_recv()
+        far_send[off] = part_sum(off, 2).astype(BF16)
+        far_copy(off, 0).start()
+        far_copy(off, 1).start()
+        return carry
+
     def send_y(off, carry):
-        core_copy(off).wait_recv()
-        for j in range(1, NY):
-            y_send[off, j - 1] = (keep[off, j] + core_recv[off, j].astype(F32)).astype(BF16)
-            remote(
-                y_send.at[off, j - 1],
-                y_recv.at[off, j - 1],
-                y_ssem,
-                y_rsem.at[off],
-                {"y": (y + j) % NY},
-            ).start()
-        keep[off, 0] = keep[off, 0] + core_recv[off, 0].astype(F32)
-        return carry
-
-    lax.fori_loop(0, NW // 2, send_y, 0)
-
+        wait_for(far_recv.at[off], far_rsem.at[off])
+        came = far_recv[off].astype(F32)
+        right, left = part_sum(off, 1), part_sum(off, 3)
+        y_send[off, 0] = jnp.concatenate(
+            [right[:quarter] + came[:quarter], right[quarter:]], axis=0
+        ).astype(BF16)
+        y_copy(off, 0).start()
+        y_send[off, 1] = jnp.concatenate(
+            [left[:quarter], left[quarter:] + came[quarter:]], axis=0
+        ).astype(BF16)
+        y_copy(off, 1).start()
+        return carry
+
+    lax.fori_loop(0, NW, send_far, 0)
     weights_on(1).wait_recv()
     weights_on(3).wait_recv()
-    UP, DOWN = NW // 2, (NW - 1) // 2
-    HV = NV // 2
-
-    def chain_up(k, part):
-        block = plane_weights.at[(w + NW - k) % NW, pl.ds(part * HV, HV)]
-        return remote(block, block, chain_send.at[0, k, part], chain_recv.at[0, k, part], up)
-
-    def chain_down(k, part):
-        block = plane_weights.at[(w + k) % NW, pl.ds(part * HV, HV)]
-        return remote(block, block, chain_send.at[1, k, part], chain_recv.at[1, k, part], down)
-
-    for part in range(2):
-        chain_up(0, part).start()
-        if DOWN:
-            chain_down(0, part).start()
-
-    def pass_on(k):
-        for part in range(2):
-            chain_up(k, part).wait_recv()
-            if k + 1 < UP:
-                chain_up(k + 1, part).start()
-            if k < DOWN:
-                chain_down(k, part).wait_recv()
-                if k + 1 < DOWN:
-                    chain_down(k + 1, part).start()
+    spread_blocks = plane_weights.at[pl.ds(0, NW - 1), 0, pl.ds(0, NX - 1)]
+    wait_for(spread_blocks, x_sems.at[3])
+    wait_for(plane_weights.at[pl.ds(0, NW - 1), 0, 0], local_sem.at[7])
+    start_chain()
+
+    lax.fori_loop(0, NW, send_y, 0)
+
+    out_copy.wait()
+    value_exchange.wait_recv()
+    values[other_half_rows, :] = val_recv[...]
+    key_part = jnp.zeros((width, T), F32)
+    for h in range(heads):
+        lanes = pl.ds(h * width, width)
+        head_grad = grad[:, lanes]
+        row_dots = jnp.sum(
+            head_grad.astype(F32) * attn_out[:, lanes].astype(F32), axis=1, keepdims=True
+        )
+        prob_grad = dot(head_grad, values[...], 1, 0)
+        score_grad = (probs[h] * (prob_grad - row_dots) * scale).astype(BF16)
+        qgrad_ref[:, lanes] = dot(score_grad, keys[...], 1, 1).astype(BF16)
+        key_part = key_part + dot(query[:, lanes], score_grad, 0, 0)
+    own_kpart = jnp.where(lower, key_part[:half], key_part[half:])
+    kpart_send[...] = jnp.where(lower, key_part[half:], key_part[:half]).astype(BF16)
+    kpart_exchange = remote(kpart_send, kpart_recv, pair_send.at[3], pair_recv.at[3], pair)
+    kpart_exchange.start()
+
+    pass_on(0)
 
     for j in (1, 3, 2):
         part_to(j).wait_recv()
@@ -347,44 +433,28 @@
         ],
         axis=1,
     )
-    plane_grads[me] = own_tokens.astype(BF16)
+    chips = NX * NY
+    plane_grads[c, x * NY + y] = own_tokens.astype(BF16)
 
     def send_grads(i, carry):
-        remote(
-            plane_grads.at[me], plane_grads.at[me], plane_sems.at[0], plane_sems.at[1], plane(i)[0]
-        ).start()
-        return carry
-
-    lax.fori_loop(1, NS, send_grads, 0)
-    lax.fori_loop(NW // 2, NW, send_y, 0)
-    pass_on(0)
-
-    out_copy.wait()
-    value_exchange.wait_recv()
-    values[other_half_rows, :] = val_recv[...]
-    key_part = jnp.zeros((width, T), F32)
-    for h in range(heads):
-        lanes = pl.ds(h * width, width)
-        head_grad = grad[:, lanes]
-        row_dots = jnp.sum(
-            head_grad.astype(F32) * attn_out[:, lanes].astype(F32), axis=1, keepdims=True
-        )
-        prob_grad = dot(head_grad, values[...], 1, 0)
-        score_grad = (probs[h] * (prob_grad - row_dots) * scale).astype(BF16)
-        qgrad_ref[:, lanes] = dot(score_grad, keys[...], 1, 1).astype(BF16)
-        key_part = key_part + dot(query[:, lanes], score_grad, 0, 0)
-    own_kpart = jnp.where(lower, key_part[:half], key_part[half:])
-    kpart_send[...] = jnp.where(lower, key_part[half:], key_part[:half]).astype(BF16)
-    kpart_exchange = remote(kpart_send, kpart_recv, pair_send.at[3], pair_recv.at[3], pair)
-    kpart_exchange.start()
-    if UP > 1:
-        pass_on(1)
+        px, py = (x + i // NY) % NX, (y + i % NY) % NY
+        block = plane_grads.at[c, x * NY + y]
+        remote(block, block, plane_sems.at[0], plane_sems.at[1], {"x": px, "y": py}).start()
+        return carry
+
+    lax.fori_loop(1, chips, send_grads, 0)
+    grads_over = remote(
+        plane_grads.at[c], plane_grads.at[c], plane_sems.at[4], plane_sems.at[5], {"c": 1 - c}
+    )
+
+    def share_grads():
+        wait_for(plane_grads.at[c, pl.ds(0, chips - 1)], plane_sems.at[1])
+        grads_over.start()
+
 
     def send_w(off):
         wait_for(y_recv.at[off], y_rsem.at[off])
-        summed = keep[off, 0]
-        for j in range(NY - 1):
-            summed = summed + y_recv[off, j].astype(F32)
+        summed = part_sum(off, 0) + y_recv[off, 0].astype(F32) + y_recv[off, 1].astype(F32)
         if off == 0:
             keep[0, 0] = summed
             return
@@ -392,35 +462,46 @@
         remote(
             w_send.at[off - 1],
             w_recv.at[off - 1],
-            w_sems.at[0],
-            w_sems.at[1],
+            w_ssem,
+            w_rsem,
             {"w": (w + off) % NW},
         ).start()
 
     pending = list(range(1, NW)) + [0]
-    share = -(-NW // UP)
-    for k in range(UP):
-        for off in pending[k * share : (k + 1) * share]:
-            send_w(off)
-        if k > 1:
-            pass_on(k)
-
-    wait_for(plane_grads.at[pl.ds(0, NS - 1)], plane_sems.at[1])
+    for off in pending[: NW // 2]:
+        send_w(off)
+    pass_on(1)
+    for off in pending[NW // 2 :]:
+        send_w(off)
+
+    share_grads()
+    for k in range(2, UP):
+        pass_on(k)
+
+    grads_over.wait_recv()
     NG = NY * NC
     pieces = []
     for d in range(2):
         acc = jnp.zeros((NG * TV, DB), F32)
         for i in range(NX):
-            left = plane_grads[i * NG : (i + 1) * NG].reshape(NG * TV, NV * half)
+            left = jnp.concatenate(
+                [
+                    plane_grads[k, i * NY : (i + 1) * NY].reshape(NY * TV, NV * half)
+                    for k in range(NC)
+                ],
+                axis=0,
+            )
             right = jnp.concatenate(
                 [plane_weights[d * RG + g, k, i] for k in range(NV) for g in range(RG)], axis=0
             )
             acc = acc + dot(left, right, 1, 0)
-        pieces.append(acc.reshape(NG, NX, TR, DB))
+        pieces.append(acc.reshape(NC, NY, NX, TR, DB))
     for i in range(NX):
-        out_send[i * NG : (i + 1) * NG] = jnp.concatenate(
-            [pieces[0][:, i], pieces[1][:, i]], axis=1
-        ).astype(BF16)
+        for j in range(NY):
+            for k in range(NC):
+                out_send[(i * NY + j) * NC + k] = jnp.concatenate(
+                    [pieces[0][k, j, i], pieces[1][k, j, i]], axis=0
+                ).astype(BF16)
 
     def send_out(i, carry):
         device, slot = plane(i)
@@ -434,7 +515,7 @@
 
     kpart_exchange.wait_recv()
     kgrad_ref[...] = (own_kpart + kpart_recv[...].astype(F32)).astype(BF16)
-    wait_for(w_recv, w_sems.at[1])
+    wait_for(w_recv, w_rsem)
     summed = keep[0, 0]
     for off in range(NW - 1):
         summed = summed + w_recv[off].astype(F32)
@@ -450,20 +531,22 @@
         weights_on(j).wait_send()
     for j in (1, 2, 3):
         part_to(j).wait_send()
-    for part in range(2):
-        for k in range(UP):
-            chain_up(k, part).wait_send()
-        for k in range(DOWN):
-            chain_down(k, part).wait_send()
+    wait_for(spread_blocks, x_sems.at[2])
+    for way, steps in enumerate((UP, DOWN)):
+        for k in range(steps):
+            for q in PIECES[way]:
+                chain(way, k, q).wait_send()
 
     def core_sent(off, carry):
         core_copy(off).wait_send()
         return carry
 
     lax.fori_loop(0, NW, core_sent, 0)
+    wait_for(far_send, far_ssem)
     wait_for(y_send, y_ssem)
-    wait_for(w_send, w_sems.at[0])
-    wait_for(plane_grads.at[pl.ds(0, NS - 1)], plane_sems.at[0])
+    wait_for(w_send, w_ssem)
+    wait_for(plane_grads.at[c, pl.ds(0, chips - 1)], plane_sems.at[0])
+    grads_over.wait_send()
     wait_for(out_send.at[pl.ds(0, NS - 1)], plane_sems.at[2])
 
 
@@ -509,6 +592,7 @@
         pltpu.VMEM((1, T), jnp.int32),
         pltpu.VMEM((T, D), BF16),
         pltpu.VMEM((half, D), BF16),
+        pltpu.VMEM((NX, R, DB), BF16),
         pltpu.VMEM((T, heads * width), BF16),
         pltpu.VMEM((T, heads * width), BF16),
         pltpu.VMEM((T, heads * width), BF16),
@@ -523,34 +607,40 @@
         half_block,
         pltpu.VMEM((NV, TV, width), BF16),
         pltpu.VMEM((NV, TV, width), BF16),
-        pltpu.VMEM((NS, TV, NV * half), BF16),
+        pltpu.VMEM((NC, NX * NY, TV, NV * half), BF16),
         pltpu.VMEM((NW, NV, NX, R, DB), BF16),
         pltpu.VMEM((NS, 2 * TR, DB), BF16),
         pltpu.VMEM((NS, 2 * TR, DB), BF16),
         pltpu.VMEM((NW, NY, half, BD), F32),
         pltpu.VMEM((NW, NY, half, BD), BF16),
         pltpu.VMEM((NW, NY, half, BD), BF16),
-        pltpu.VMEM((NW, NY - 1, half, BD), BF16),
-        pltpu.VMEM((NW, NY - 1, half, BD), BF16),
+        pltpu.VMEM((NW, half, BD), BF16),
+        pltpu.VMEM((NW, half, BD), BF16),
+        pltpu.VMEM((NW, 2, half, BD), BF16),
+        pltpu.VMEM((NW, 2, half, BD), BF16),
         pltpu.VMEM((NW - 1, half, BD), BF16),
         pltpu.VMEM((NW - 1, half, BD), BF16),
         dma((8,)),
         dma((4,)),
+        dma((NX,)),
         dma((4,)),
         dma((4,)),
-        dma((2,)),
+        dma((4,)),
         dma((NV,)),
         dma((NV,)),
         dma((NV,)),
         dma((NV,)),
-        dma((2, NW, 2)),
-        dma((2, NW, 2)),
-        dma((4,)),
+        dma((2, NW // 2, NV)),
+        dma((2, NW // 2, NV)),
+        dma((6,)),
         dma((NW,)),
         dma((NW,)),
         dma,
         dma((NW,)),
-        dma((2,)),
+        dma,
+        dma((NW,)),
+        dma,
+        dma,
     ]
     anywhere = pl.BlockSpec(memory_space=pltpu.HBM)
     vmem = pl.BlockSpec(memory_space=pltpu.VMEM)

time: 86.2 us -> 82.3 us (0.955)
  Pallas kernels: 85.4 us -> 81.5 us
    pallas_call x1, Pallas kernels: 84.6 us -> 80.6 us  [per_device(): pl.pallas_call(functools.partial(kernel, sizes), out_shape=(jax.ShapeDtyp...]
where the time goes in v3:
time: 82.3 us; the launch traced here: 82.1 us
  Pallas kernels  81.5 us (99%)
    pallas_call x1, Pallas kernels, per_device(): pl.pallas_call(functools.partial(kernel, sizes), out_shape=(jax.ShapeDtyp...  80.6 us

profile of v3, /device:TPU:1, one launch (start us, length us, event | category | flops | bytes accessed | tf_op | source)
XLA Modules:
  0.0 82.1 jit_solution(3513302472761524354)
XLA Ops:
  0.6 80.6 %shard_map.111 = (bf16[128,1024]{1,0:T(8,128)(2,1)S(1)}, bf16[64,128]{1,0:T(8,128)(2,1)S(1)}, bf16[32,16,256]{2,1,0:T(8,128)(2,1)S(1)}, f32[64,256]{1,0:T(8,128)S(1)}) custom-call(bf16[128,16384]{1,0:T(8,128)(2,1)} %bitcast.21, bf16[64,16384]{1,0:T(8,128)(2,1)} %bitcast.22, bf16[128,1024]{1,0:T(8,128)(2,1)} %bitcast.23, bf16[64,128]{1,0:T(8,128)(2,1)} %bitcast.26, ...), custom_call_target="tpu_custom_call" | custom-call | tf_op jit(solution)/shard_map/pallas_call | solution.py:647
  81.3 0.8 %shard_map.112 = (bf16[128,1024]{1,0:T(8,128)(2,1)}, bf16[64,128]{1,0:T(8,128)(2,1)}, bf16[32,16,256]{2,1,0:T(8,128)(2,1)}, f32[64,256]{1,0:T(8,128)}) custom-call(bf16[128,1024]{1,0:T(8,128)(2,1)S(1)} %get-tuple-element.12.refs_0_, bf16[64,128]{1,0:T(8,128)(2,1)S(1)} %get-tuple-element.13.refs_1_, bf16[32,16,256]{2,1,0:T(8,128)(2,1)S(1)} %get-tuple-element.14.refs_2_, ...), custom_call_target="tpu_custom_call" | custom-call | tf_op jit(solution)/shard_map/pallas_call | solution.py:676

commit v4 on v3

--- a/solution.py
+++ b/solution.py
@@ -112,6 +112,7 @@
         px, py, pc = (x + dx) % NX, (y + dy) % NY, (c + dc) % NC
         return {"x": px, "y": py, "c": pc}, (px * NY + py) * NC + pc
 
+    beside = w + 1 - 2 * (w % 2)
     position = v * NW + w
     after, before = (position + 1) % (NV * NW), (position + NV * NW - 1) % (NV * NW)
     up = {"v": after // NW, "w": after % NW}
@@ -185,16 +186,14 @@
 
     lax.fori_loop(1, NS, greet_plane, 0)
 
-    def greet_line(i, carry):
-        greet({"w": (w + i) % NW})
-        return carry
-
-    lax.fori_loop(1, NW, greet_line, 0)
+    for i in range(1, NW // 2):
+        greet({"w": (w + 2 * i) % NW})
+    greet({"w": beside})
 
     key_copy.wait()
     for copy in piece_copies:
         copy.wait()
-    pl.semaphore_wait(barrier, 4 + (NS - 1) + (NW - 1))
+    pl.semaphore_wait(barrier, 4 + (NS - 1) + NW // 2)
 
     key_exchange = remote(keys.at[own_half_rows], key_recv, pair_send.at[0], pair_recv.at[0], pair)
     key_exchange.start()
@@ -335,8 +334,9 @@
             {"c": 1 - c},
         )
 
-    def make_blocks(off, carry):
-        to_w = (w + off) % NW
+    def make_blocks(turn, carry):
+        off = (2 * turn + 1) % (NW + 1)
+        to_w = (w + off % 2 * (beside - w) + off // 2 * 2) % NW
         for j in range(NY):
             block = (((y + j) % NY) * NW + to_w) * NC
             own = pl.multiple_of((block + c) * BD, BD)
@@ -372,14 +372,16 @@
             {"y": (y + (1, NY - 1)[way]) % NY},
         )
 
-    def send_far(off, carry):
+    def send_far(turn, carry):
+        off = (2 * turn + 1) % (NW + 1)
         core_copy(off).wait_recv()
         far_send[off] = part_sum(off, 2).astype(BF16)
         far_copy(off, 0).start()
         far_copy(off, 1).start()
         return carry
 
-    def send_y(off, carry):
+    def send_y(turn, carry):
+        off = (2 * turn + 1) % (NW + 1)
         wait_for(far_recv.at[off], far_rsem.at[off])
         came = far_recv[off].astype(F32)
         right, left = part_sum(off, 1), part_sum(off, 3)
@@ -452,28 +454,26 @@
         grads_over.start()
 
 
-    def send_w(off):
+    PAIRS = NW // 2
+
+    def y_sum(off):
         wait_for(y_recv.at[off], y_rsem.at[off])
-        summed = part_sum(off, 0) + y_recv[off, 0].astype(F32) + y_recv[off, 1].astype(F32)
-        if off == 0:
-            keep[0, 0] = summed
-            return
-        w_send[off - 1] = summed.astype(BF16)
-        remote(
-            w_send.at[off - 1],
-            w_recv.at[off - 1],
-            w_ssem,
-            w_rsem,
-            {"w": (w + off) % NW},
-        ).start()
-
-    pending = list(range(1, NW)) + [0]
-    for off in pending[: NW // 2]:
-        send_w(off)
+        return part_sum(off, 0) + y_recv[off, 0].astype(F32) + y_recv[off, 1].astype(F32)
+
+    def w_copy(slot, step, to):
+        return remote(
+            w_send.at[slot], w_recv.at[slot], w_ssem, w_rsem.at[step], {"w": to}
+        )
+
+    for i in range(PAIRS):
+        w_send[i] = y_sum(2 * i + 1).astype(BF16)
+        w_copy(i, 0, beside).start()
     pass_on(1)
-    for off in pending[NW // 2 :]:
-        send_w(off)
-
+    wait_for(w_recv.at[pl.ds(0, PAIRS)], w_rsem.at[0])
+    for i in range(1, PAIRS):
+        w_send[PAIRS + i - 1] = (y_sum(2 * i) + w_recv[i].astype(F32)).astype(BF16)
+        w_copy(PAIRS + i - 1, 1, (w + 2 * i) % NW).start()
+    own_sum = y_sum(0) + w_recv[0].astype(F32)
     share_grads()
     for k in range(2, UP):
         pass_on(k)
@@ -515,10 +515,10 @@
 
     kpart_exchange.wait_recv()
     kgrad_ref[...] = (own_kpart + kpart_recv[...].astype(F32)).astype(BF16)
-    wait_for(w_recv, w_rsem)
-    summed = keep[0, 0]
-    for off in range(NW - 1):
-        summed = summed + w_recv[off].astype(F32)
+    wait_for(w_recv.at[pl.ds(PAIRS, PAIRS - 1)], w_rsem.at[1])
+    summed = own_sum
+    for i in range(PAIRS, NW - 1):
+        summed = summed + w_recv[i].astype(F32)
     wgrad_ref[...] = summed
     wait_for(out_recv.at[pl.ds(0, NS - 1)], plane_sems.at[3])
     igrad_ref[...] = out_recv[...]
@@ -640,7 +640,7 @@
         dma,
         dma((NW,)),
         dma,
-        dma,
+        dma((2,)),
     ]
     anywhere = pl.BlockSpec(memory_space=pltpu.HBM)
     vmem = pl.BlockSpec(memory_space=pltpu.VMEM)

time: 82.3 us -> 81.1 us (0.985)
  Pallas kernels: 81.5 us -> 80.3 us
    pallas_call x1, Pallas kernels: 80.6 us -> 79.4 us  [per_device(): pl.pallas_call(functools.partial(kernel, sizes), out_shape=(jax.ShapeDtyp...]
where the time goes in v4:
time: 81.1 us; the launch traced here: 80.9 us
  Pallas kernels  80.3 us (99%)
    pallas_call x1, Pallas kernels, per_device(): pl.pallas_call(functools.partial(kernel, sizes), out_shape=(jax.ShapeDtyp...  79.4 us

profile of v4, /device:TPU:1, one launch (start us, length us, event | category | flops | bytes accessed | tf_op | source)
XLA Modules:
  0.0 80.9 jit_solution(18420025456596220089)
XLA Ops:
  0.6 79.4 %shard_map.111 = (bf16[128,1024]{1,0:T(8,128)(2,1)S(1)}, bf16[64,128]{1,0:T(8,128)(2,1)S(1)}, bf16[32,16,256]{2,1,0:T(8,128)(2,1)S(1)}, f32[64,256]{1,0:T(8,128)S(1)}) custom-call(bf16[128,16384]{1,0:T(8,128)(2,1)} %bitcast.21, bf16[64,16384]{1,0:T(8,128)(2,1)} %bitcast.22, bf16[128,1024]{1,0:T(8,128)(2,1)} %bitcast.23, bf16[64,128]{1,0:T(8,128)(2,1)} %bitcast.26, ...), custom_call_target="tpu_custom_call" | custom-call | tf_op jit(solution)/shard_map/pallas_call | solution.py:647
  80.1 0.8 %shard_map.112 = (bf16[128,1024]{1,0:T(8,128)(2,1)}, bf16[64,128]{1,0:T(8,128)(2,1)}, bf16[32,16,256]{2,1,0:T(8,128)(2,1)}, f32[64,256]{1,0:T(8,128)}) custom-call(bf16[128,1024]{1,0:T(8,128)(2,1)S(1)} %get-tuple-element.12.refs_0_, bf16[64,128]{1,0:T(8,128)(2,1)S(1)} %get-tuple-element.13.refs_1_, bf16[32,16,256]{2,1,0:T(8,128)(2,1)S(1)} %get-tuple-element.14.refs_2_, ...), custom_call_target="tpu_custom_call" | custom-call | tf_op jit(solution)/shard_map/pallas_call | solution.py:676
